TPU v7x, 128 devices: a whole 4x4x4 slice. The times are simulated.
128 devices in a mesh: sub: 32 (over z, y, core), rve: 4 (over x).
Axes of the slice: x: 4, y: 4, z: 4, core: 2. Of those that a mesh axis runs over, the one named last changes fastest.
Arguments:
- displacement: float32 [3, 32, 8, 8], P(None, 'sub', 'rve'), may hold values from -4 to 4
- load: float32 [3, 32, 8, 8], P(None, 'sub', 'rve'), may hold values from -6 to 6
- home_slot: int32 [16384], P(('sub', 'rve')), may hold values from 0 to 16383, as said below
- micro_state: float32 [7, 3, 216, 16384], P(None, None, None, ('sub', 'rve')), may hold values from -6 to 6
- state_slot: int32 [16384], P(('sub', 'rve')), may hold values from 0 to 16383, as said below
- phases: int32 [216, 16384], P(None, ('sub', 'rve')), may hold values from 0 to 2
- phase_moduli: float32 [2, 3], replicated, may hold values from 0.5 to 8
Outputs:
- new_state: float32 [7, 3, 216, 16384], P(None, None, None, ('sub', 'rve'))
- displaced: float32 [3, 32, 8, 8], P(None, 'sub', 'rve')
- residual: float32 [3, 32, 8, 8], P(None, 'sub', 'rve')
- rel_norm: float32 [], replicated
Inputs may be any that keep to these rules, and one draw needn't show every extreme that they name: `home_slot`: A permutation of 0 to 16383. The 128 entries held by device s (devices numbered in sub+rve order) contain, for every device d, exactly one value, d * 128 + s, in an order drawn at random; so each device sends exactly one Gauss point to every device. `state_slot`: A permutation of 0 to 16383 with the same structure: the 128 entries held by device s contain, for every device d, exactly one value, d * 128 + s, in an order drawn at random.
All inputs are finite; a program needn't handle non-finite values.
Results may differ from a plain program's by a relative error of at most 0.0003.
Values sent between devices are 32-bit elements; how exact they have to be, the bound alone decides.
A program may use at most 128 MiB of HBM per device.

v0:
```python
import functools
import math

import jax
import jax.numpy as jnp
import numpy as np
from jax import lax
from jax.experimental import pallas as pl
from jax.experimental.pallas import tpu as pltpu
from jax.sharding import PartitionSpec as P

R = 6
VOX = 216
CASES = 7
STAB = 0.1
FLOOR = 1.0
NDEV = 128
NRVE = 4
NSUB = 32
ROWS = CASES * 3 * VOX
CASE_ROWS = 3 * VOX
CHUNKS = (8, 8, 8, 8, 4)
FIRST = (0, 8, 16, 24, 32)
CHUNK_AT = {0: 0, 1: 1, 3: 2, 4: 3, 6: 4}
CELLS = 36
MESH = pl.DeviceIdType.MESH
F32 = jnp.float32
TERMS = (((0, 0), (2, 4), (1, 5)), ((1, 1), (2, 3), (0, 5)), ((2, 2), (1, 3), (0, 4)))


def tables():
    offset = 0.5 / math.sqrt(3.0)
    places = (0.5 - offset, 0.5 + offset)
    slopes = np.zeros((3, 8, NDEV), np.float32)
    for g in range(NDEV):
        q = g % 8
        at = (places[q % 2], places[q // 2 % 2], places[q // 4])
        for a in range(8):
            bits = (a % 2, a // 2 % 2, a // 4)
            w = [at[k] if bits[k] else 1.0 - at[k] for k in range(3)]
            s = [1.0 if bits[k] else -1.0 for k in range(3)]
            slopes[0, a, g] = s[0] * w[1] * w[2]
            slopes[1, a, g] = w[0] * s[1] * w[2]
            slopes[2, a, g] = w[0] * w[1] * s[2]
    mask = np.zeros((8, NDEV), np.float32)
    pick = np.zeros((8, NDEV), np.int32)
    for n in range(48):
        nz, ny, nx = n // 24, n // 8 % 3, n % 8
        for a in range(8):
            ax, ay, az = a % 2, a // 2 % 2, a // 4
            ly = ny - ay
            if az == nz and 0 <= ly < 2:
                mask[a, n] = 1.0
                pick[a, n] = (ly * 8 + (nx - ax) % 8) * 8
    corner = np.zeros((8, NDEV), np.int32)
    for g in range(NDEV):
        ly, ex = g // 64, g // 8 % 8
        for a in range(8):
            ax, ay, az = a % 2, a // 2 % 2, a // 4
            corner[a, g] = az * 24 + (ly + ay) * 8 + (ex + ax) % 8
    floats = np.concatenate([slopes.reshape(24, NDEV), mask], axis=0)
    ints = np.concatenate([pick, corner], axis=0)
    return floats, ints


def dev(d):
    return (d // NRVE, lax.rem(d, NRVE))


def lanes(x, index):
    return jnp.take_along_axis(x, index, axis=1, mode="promise_in_bounds")


def sublanes(x, index):
    return jnp.take_along_axis(x, index, axis=0, mode="promise_in_bounds")


def spread(row):
    return jnp.broadcast_to(row, (8, NDEV))


def inverse(target):
    column = jnp.broadcast_to(target, (NDEV, NDEV)).T
    lane = lax.broadcasted_iota(jnp.int32, (NDEV, NDEV), 1)
    row = lax.broadcasted_iota(jnp.int32, (NDEV, NDEV), 0)
    return jnp.sum(jnp.where(column == lane, row, 0).astype(F32), axis=0, keepdims=True).astype(jnp.int32)


def kernel(
    disp_ref, load_ref, home_ref, state_slot_ref, moduli_ref, micro_ref, phase_ref, float_ref, int_ref,
    new_ref, displaced_ref, residual_ref, norm_ref,
    xin, ph, send0, send1, send2, send3, send4, recv0, recv1, recv2, recv3, recv4,
    nat, outb, lam, mu, w, p0, p1, ap, sig, sums, av, ret_out, ret_in, dtile, dhalo, ntile, nhalo, nrow, nall,
    in_sem, ph_sem, out_sem, local_sem, send_sem, recv_sem, near_send, near_recv,
):
    sub, rve = lax.axis_index("sub"), lax.axis_index("rve")
    me = sub * NRVE + rve
    sends = (send0, send1, send2, send3, send4)
    recvs = (recv0, recv1, recv2, recv3, recv4)

    barrier = pltpu.get_barrier_semaphore()

    @pl.loop(1, NDEV)
    def _(k):
        pl.semaphore_signal(barrier, inc=1, device_id=dev(lax.rem(me + k, NDEV)), device_id_type=MESH)

    loads = []
    for position in range(CASES):
        case = (position + 1) % CASES
        copy = pltpu.make_async_copy(
            micro_ref.at[pl.ds(case * CASE_ROWS, CASE_ROWS)],
            xin.at[pl.ds(position * CASE_ROWS, CASE_ROWS)],
            in_sem.at[position],
        )
        copy.start()
        loads.append(copy)
    phase_load = pltpu.make_async_copy(phase_ref, ph.at[pl.ds(0, VOX)], ph_sem)
    phase_load.start()

    dtile[...] = jnp.zeros((8, NDEV), F32)
    for i in range(3):
        for y in range(2):
            dtile[i : i + 1, 8 * y : 8 * y + 8] = disp_ref[i, 0, y : y + 1, :]

    home_dev = lax.shift_right_logical(home_ref[...], 7)
    state_index = spread(inverse(lax.shift_right_logical(state_slot_ref[...], 7)))
    home_index = spread(inverse(home_dev))

    def prepare(chunk, row, last):
        base = pl.multiple_of((FIRST[chunk] + row) * NDEV, NDEV)
        parts = []
        for i in range(16):
            if last and i > 7:
                parts.append(jnp.zeros((8, NDEV), F32))
            else:
                block = xin[pl.ds(base + 8 * i, 8), :]
                parts.append(lanes(block, home_index if last and i == 7 else state_index))
        pitch = CHUNKS[chunk]
        sends[chunk][pl.ds(row, NDEV, stride=pitch), :] = jnp.concatenate(parts, axis=0).T

    def prepare_chunk(chunk):
        rows = CHUNKS[chunk]
        if chunk < 4:
            for row in range(rows):
                prepare(chunk, row, False)
        else:
            for row in range(rows):
                prepare(chunk, row, row == rows - 1)

    def send_chunk(chunk):
        rows = CHUNKS[chunk]
        own = pl.ds(pl.multiple_of(me * rows, rows), rows)

        @pl.loop(1, NDEV)
        def _(k):
            d = lax.rem(me + k, NDEV)
            pltpu.make_async_remote_copy(
                src_ref=sends[chunk].at[pl.ds(pl.multiple_of(d * rows, rows), rows)],
                dst_ref=recvs[chunk].at[own],
                send_sem=send_sem.at[chunk],
                recv_sem=recv_sem.at[chunk],
                device_id=dev(d),
                device_id_type=MESH,
            ).start()

        pltpu.make_async_copy(sends[chunk].at[own], recvs[chunk].at[own], local_sem.at[chunk]).start()

    def whole(src, dst, rows, index):
        return pltpu.make_async_remote_copy(
            src_ref=src.at[pl.ds(0, (NDEV - 1) * rows)],
            dst_ref=dst.at[pl.ds(0, (NDEV - 1) * rows)],
            send_sem=send_sem.at[index],
            recv_sem=recv_sem.at[index],
            device_id=dev(lax.rem(me + 1, NDEV)),
            device_id_type=MESH,
        )

    for position in (0, 1):
        loads[position].wait()
    prepare_chunk(0)

    pl.semaphore_wait(barrier, NDEV - 1)

    def near(index, src, dst, dsub, drve):
        to_sub = lax.rem(sub + dsub + NSUB, NSUB)
        to_rve = lax.rem(rve + drve + NRVE, NRVE)
        return pltpu.make_async_remote_copy(
            src_ref=src,
            dst_ref=dst,
            send_sem=near_send.at[index],
            recv_sem=near_recv.at[index],
            device_id=(to_sub, to_rve),
            device_id_type=MESH,
        )

    steps = ((0, 1), (1, 0), (1, 1))
    halo_in = [near(i, dtile, dhalo.at[i], -s, -r) for i, (s, r) in enumerate(steps)]
    for copy in halo_in:
        copy.start()
    send_chunk(0)
    for position in (2, 3):
        loads[position].wait()
    prepare_chunk(1)
    send_chunk(1)
    loads[4].wait()
    prepare_chunk(2)
    send_chunk(2)
    for position in (5, 6):
        loads[position].wait()
    prepare_chunk(3)
    send_chunk(3)

    for copy in halo_in:
        copy.wait()
    lane = lax.broadcasted_iota(jnp.int32, (8, NDEV), 1)
    row8 = lax.broadcasted_iota(jnp.int32, (8, NDEV), 0)
    below = jnp.where(sub < NSUB - 1, 1.0, 0.0).astype(F32)
    extended = dtile[...]
    extended = jnp.where((lane >= 16) & (lane < 24), pltpu.roll(dhalo[0], 16, axis=1), extended)
    extended = jnp.where((lane >= 24) & (lane < 40), pltpu.roll(dhalo[1], 24, axis=1) * below, extended)
    extended = jnp.where((lane >= 40) & (lane < 48), pltpu.roll(dhalo[2], 40, axis=1) * below, extended)
    slope = [jnp.zeros((8, NDEV), F32) for _ in range(3)]
    for a in range(8):
        value = lanes(extended, spread(int_ref[8 + a : 9 + a, :]))
        for k in range(3):
            slope[k] = slope[k] + float_ref[8 * k + a : 8 * k + a + 1, :] * value
    s0, s1, s2 = slope
    strains = [
        s0[0:1], s1[1:2], s2[2:3],
        s2[1:2] + s1[2:3], s2[0:1] + s0[2:3], s1[0:1] + s0[1:2],
    ]
    strain_rows = jnp.zeros((8, NDEV), F32)
    for m in range(6):
        strain_rows = jnp.where(row8 == m, spread(strains[m]), strain_rows)
    xin[pl.ds(ROWS, 8), :] = strain_rows
    prepare_chunk(4)
    send_chunk(4)

    phase_load.wait()
    ph[pl.ds(VOX, 8), :] = jnp.zeros((8, NDEV), jnp.int32)
    inside = row8 < R

    @pl.loop(0, CELLS)
    def _(cell):
        label = ph[pl.ds(cell * R, 8), :]
        for which, out in ((0, lam), (1, mu)):
            value = jnp.where(
                label == 0,
                moduli_ref[which, 0],
                jnp.where(label == 1, moduli_ref[which, 1], moduli_ref[which, 2]),
            )
            out[cell] = jnp.where(inside, value, 0.0)

    av[...] = jnp.zeros((NDEV, NDEV), F32)
    up = jnp.where(row8 < 5, row8 + 1, jnp.where(row8 == 5, 0, row8))
    down = jnp.where(row8 == 0, 5, jnp.where(row8 < 6, row8 - 1, row8))

    def receive(chunk):
        rows = CHUNKS[chunk]
        own = pl.ds(pl.multiple_of(me * rows, rows), rows)
        whole(sends[chunk], recvs[chunk], rows, chunk).wait_recv()
        pltpu.make_async_copy(sends[chunk].at[own], recvs[chunk].at[own], local_sem.at[chunk]).wait()
        for row in range(rows):
            block = recvs[chunk][pl.ds(row, NDEV, stride=rows), :]
            nat[pl.ds((FIRST[chunk] + row) * NDEV, NDEV), :] = block.T

    zero = jnp.zeros((8, NDEV), F32)

    def stress_at(src, a, b, applied):
        following = lax.rem(a + 1, R)
        g = []
        for i in range(3):
            here = src[i * CELLS + a * R + b]
            g.append(
                (
                    src[i * CELLS + following * R + b] - here,
                    src[i * CELLS + a * R + (b + 1) % R] - here,
                    sublanes(here, up) - here,
                )
            )
        eps = [g[0][0], g[1][1], g[2][2], g[1][2] + g[2][1], g[0][2] + g[2][0], g[0][1] + g[1][0]]
        if applied is not None:
            eps = [eps[m] + applied[m] for m in range(6)]
        cell = a * R + b
        first, second = lam[cell], mu[cell]
        volume = first * (eps[0] + eps[1] + eps[2])
        twice = second + second
        stress = [volume + twice * eps[m] for m in range(3)] + [second * eps[m] for m in range(3, 6)]
        return stress, eps

    def stresses(src, applied):
        def body(a, total):
            total = list(total)
            for b in range(R):
                stress, _ = stress_at(src, a, b, applied)
                for m in range(6):
                    sig[m * CELLS + a * R + b] = stress[m]
                    total[m] = total[m] + stress[m]
            return tuple(total)

        return lax.fori_loop(0, R, body, (zero,) * 6)

    voigt = ((0, 5, 4), (5, 1, 3), (4, 3, 2))

    def force_at(src, a, b):
        before = lax.rem(a + R - 1, R)
        cell = a * R + b
        here = [sig[m * CELLS + cell] for m in range(6)]
        out = []
        for i in range(3):
            total = sig[voigt[0][i] * CELLS + before * R + b] - here[voigt[0][i]]
            total = total + (sig[voigt[1][i] * CELLS + a * R + (b + R - 1) % R] - here[voigt[1][i]])
            last = here[voigt[2][i]]
            total = total + (sublanes(last, down) - last)
            out.append(total + STAB * src[i * CELLS + cell])
        return out

    def across(x):
        return spread(jnp.sum(x, axis=0, keepdims=True))

    def case_body(position, carry):
        for when, chunk in CHUNK_AT.items():

            @pl.when(position == when)
            def _():
                receive(chunk)

        case = lax.rem(position + 1, CASES)
        macro = nat[pl.ds(ROWS, 8), :]
        applied = []
        for m in range(6):
            unit = jnp.where(position == m, 1.0, 0.0).astype(F32)
            applied.append(jnp.where(position == CASES - 1, spread(macro[m : m + 1, :]), unit))

        @pl.loop(0, CELLS)
        def _(cell):
            for i in range(3):
                at = position * CASE_ROWS + i * VOX + cell * R
                w[i * CELLS + cell] = jnp.where(inside, nat[pl.ds(at, 8), :], 0.0)

        total0 = stresses(w, applied)

        def first(a, rr):
            for b in range(R):
                force = force_at(w, a, b)
                for i in range(3):
                    value = -force[i]
                    p0[i * CELLS + a * R + b] = value
                    rr = rr + value * value
            return rr

        rr = across(lax.fori_loop(0, R, first, zero))
        total1 = stresses(p0, None)

        def second(a, curve):
            for b in range(R):
                force = force_at(p0, a, b)
                for i in range(3):
                    ap[i * CELLS + a * R + b] = force[i]
                    curve = curve + p0[i * CELLS + a * R + b] * force[i]
            return curve

        alpha0 = rr / across(lax.fori_loop(0, R, second, zero))

        def reduce(a, total):
            for j in range(3 * R):
                at = a * (3 * R) + j
                value = p0[at] - alpha0 * ap[at]
                p1[at] = value
                total = total + value * value
            return total

        rn = across(lax.fori_loop(0, R, reduce, zero))
        beta = rn / rr

        @pl.loop(0, R)
        def _(a):
            for j in range(3 * R):
                at = a * (3 * R) + j
                p1[at] = p1[at] + beta * p0[at]

        def third(a, carried):
            curve, total = carried[0], list(carried[1:])
            for b in range(R):
                stress, eps = stress_at(p1, a, b, None)
                for m in range(6):
                    total[m] = total[m] + stress[m]
                    curve = curve + stress[m] * eps[m]
                for i in range(3):
                    here = p1[i * CELLS + a * R + b]
                    curve = curve + (STAB * here) * here
            return (curve, *total)

        found = lax.fori_loop(0, R, third, (zero,) * 7)
        alpha1 = rn / across(found[0])
        for m in range(6):
            mean = jnp.sum(total0[m] + alpha0 * total1[m] + alpha1 * found[1 + m], axis=0, keepdims=True)
            av[pl.ds(case * 6 + m, 1), :] = mean * (1.0 / VOX)

        @pl.loop(0, CELLS)
        def _(cell):
            for i in range(3):
                at = i * CELLS + cell
                value = w[at] + alpha0 * p0[at] + alpha1 * p1[at]
                outb[pl.ds(case * CASE_ROWS + i * VOX + cell * R, R), :] = value[0:R, :]

        span = pl.ds(pl.multiple_of(case * CASE_ROWS, 8), CASE_ROWS)
        pltpu.make_async_copy(outb.at[span], new_ref.at[span], out_sem).start()
        return carry

    lax.fori_loop(0, CASES, case_body, 0)

    def send_rows(src, dst, rows, index):
        own = pl.ds(me * rows, rows)

        @pl.loop(1, NDEV)
        def _(k):
            d = lax.rem(me + k, NDEV)
            pltpu.make_async_remote_copy(
                src_ref=src.at[pl.ds(d * rows, rows)] if index == 5 else src,
                dst_ref=dst.at[own],
                send_sem=send_sem.at[index],
                recv_sem=recv_sem.at[index],
                device_id=dev(d),
                device_id_type=MESH,
            ).start()

    ret_out[...] = av[...].T
    send_rows(ret_out, ret_in, 1, 5)
    own_row = pl.ds(me, 1)
    own_copy = pltpu.make_async_copy(ret_out.at[own_row], ret_in.at[own_row], local_sem.at[5])
    own_copy.start()
    load_rows = zero
    for i in range(3):
        for y in range(2):
            dhalo[3, i : i + 1, 8 * y : 8 * y + 8] = load_ref[i, 0, y : y + 1, :]
    load_rows = jnp.where((lane < 16) & (row8 < 3), dhalo[3], 0.0)
    load_square = jnp.sum(load_rows * load_rows, keepdims=True)
    whole(ret_out, ret_in, 1, 5).wait_recv()
    own_copy.wait()
    back = ret_in[...].T
    home_rows = spread(home_dev)
    at_home = [lanes(back[8 * i : 8 * i + 8, :], home_rows) for i in range(6)]

    def averaged(case, m):
        row = case * 6 + m
        return at_home[row // 8][row % 8 : row % 8 + 1, :]

    grad = [float_ref[8 * k : 8 * k + 8, :] for k in range(3)]
    pick, mask = int_ref[0:8, :], float_ref[24:32, :]
    node_rows = []
    for kind in range(2):
        for i in range(3):
            value = zero
            for k, m in TERMS[i]:
                if kind == 0:
                    inner = spread(averaged(0, m))
                else:
                    inner = zero
                    for l, j in TERMS[i]:
                        inner = inner + grad[l] * averaged(1 + j, m)
                value = value + grad[k] * inner
            for step in (1, 2, 4):
                value = value + pltpu.roll(value, NDEV - step, axis=1)
            value = lanes(value, pick) * (mask * 0.125)
            node_rows.append(jnp.sum(value, axis=0, keepdims=True))
    tile = zero
    for r, value in enumerate(node_rows):
        tile = jnp.where(row8 == r, spread(value), tile)
    ntile[...] = tile
    part = load_rows - jnp.where(row8 < 3, tile, 0.0)
    first_row = part[0:1] + pltpu.roll(part[1:2], 64, axis=1)
    second_row = jnp.where(lane[0:1] == NDEV - 1, jnp.broadcast_to(load_square, (1, NDEV)), part[2:3])
    nrow[...] = jnp.concatenate([first_row, second_row], axis=0)
    nall[pl.ds(me * 2, 2), :] = jnp.concatenate([first_row, second_row], axis=0)
    halo_out = [near(3 + i, ntile, nhalo.at[i], s, r) for i, (s, r) in enumerate(steps)]
    for copy in halo_out:
        copy.start()
    send_rows(nrow, nall, 2, 6)

    for copy in halo_out:
        copy.wait()
    above = jnp.where(sub > 0, 1.0, 0.0).astype(F32)
    node = jnp.where(lane < 16, tile, 0.0)
    node = node + jnp.where(lane < 8, pltpu.roll(nhalo[0], NDEV - 16, axis=1), 0.0)
    node = node + jnp.where(lane < 16, pltpu.roll(nhalo[1], NDEV - 24, axis=1) * above, 0.0)
    node = node + jnp.where(lane < 8, pltpu.roll(nhalo[2], NDEV - 40, axis=1) * above, 0.0)
    residual = load_rows[0:3] - node[0:3]
    moved = dtile[0:3, :] + residual / jnp.maximum(node[3:6], FLOOR)
    for i in range(3):
        for y in range(2):
            displaced_ref[i, 0, y : y + 1, :] = moved[i : i + 1, 8 * y : 8 * y + 8]
            residual_ref[i, 0, y : y + 1, :] = residual[i : i + 1, 8 * y : 8 * y + 8]

    pltpu.make_async_remote_copy(
        src_ref=nall.at[pl.ds(0, 2 * NDEV - 2)],
        dst_ref=nall.at[pl.ds(0, 2 * NDEV - 2)],
        send_sem=send_sem.at[6],
        recv_sem=recv_sem.at[6],
        device_id=dev(lax.rem(me + 1, NDEV)),
        device_id_type=MESH,
    ).wait_recv()
    turn = jnp.where(lax.rem(row8, 4) == 0, row8 + 3, row8 - 1)
    square = zero
    load_sum = zero
    low = lax.rem(lane, 64)
    for half in range(2):
        before_z = zero
        for block in range(16):
            value = nall[pl.ds(block * 16 + half, 8, stride=2), :]
            if half == 1:
                load_sum = load_sum + jnp.where(lane == NDEV - 1, value, 0.0)
                value = jnp.where(lane < 64, value, 0.0)
            other = pltpu.roll(sublanes(value, turn), NDEV - 16, axis=1)
            value = value + jnp.where((low < 8) | ((low >= 24) & (low < 32)), other, 0.0)
            plane = pltpu.roll(value, NDEV - 24, axis=1)
            shifted = jnp.where(row8 < 4, pltpu.roll(before_z, 4, axis=0), pltpu.roll(plane, 4, axis=0))
            before_z = plane
            value = jnp.where(low < 16, value + shifted, 0.0)
            square = square + value * value
    norm_ref[...] = jnp.sqrt(jnp.sum(square, keepdims=True) / jnp.sum(load_sum, keepdims=True))

    for chunk in range(5):
        whole(sends[chunk], recvs[chunk], CHUNKS[chunk], chunk).wait_send()
    whole(ret_out, ret_in, 1, 5).wait_send()
    pltpu.make_async_remote_copy(
        src_ref=nall.at[pl.ds(0, 2 * NDEV - 2)],
        dst_ref=nall.at[pl.ds(0, 2 * NDEV - 2)],
        send_sem=send_sem.at[6],
        recv_sem=recv_sem.at[6],
        device_id=dev(lax.rem(me + 1, NDEV)),
        device_id_type=MESH,
    ).wait_send()
    pltpu.make_async_copy(outb, new_ref, out_sem).wait()


def per_device(displacement, load, home_slot, micro_state, state_slot, phases, phase_moduli):
    floats, ints = tables()
    vmem = pl.BlockSpec(memory_space=pltpu.VMEM)
    smem = pl.BlockSpec(memory_space=pltpu.SMEM)
    hbm = pl.BlockSpec(memory_space=pl.ANY)
    buffers = [pltpu.VMEM((NDEV * rows, NDEV), F32) for rows in CHUNKS]
    cells = pltpu.VMEM((3 * CELLS, 8, NDEV), F32)
    dma = pltpu.SemaphoreType.DMA
    new_state, displaced, residual, norm = pl.pallas_call(
        kernel,
        out_shape=(
            jax.ShapeDtypeStruct((ROWS, NDEV), F32),
            jax.ShapeDtypeStruct(displacement.shape, F32),
            jax.ShapeDtypeStruct(displacement.shape, F32),
            jax.ShapeDtypeStruct((1, 1), F32),
        ),
        in_specs=[vmem, vmem, vmem, vmem, smem, hbm, hbm, vmem, vmem],
        out_specs=(hbm, vmem, vmem, vmem),
        scratch_shapes=[
            pltpu.VMEM((ROWS + 72, NDEV), F32),
            pltpu.VMEM((VOX + 8, NDEV), jnp.int32),
            *buffers,
            *buffers,
            pltpu.VMEM((ROWS + 72, NDEV), F32),
            pltpu.VMEM((ROWS, NDEV), F32),
            pltpu.VMEM((CELLS, 8, NDEV), F32),
            pltpu.VMEM((CELLS, 8, NDEV), F32),
            cells,
            cells,
            cells,
            cells,
            pltpu.VMEM((6 * CELLS, 8, NDEV), F32),
            pltpu.VMEM((12, 8, NDEV), F32),
            pltpu.VMEM((NDEV, NDEV), F32),
            pltpu.VMEM((NDEV, NDEV), F32),
            pltpu.VMEM((NDEV, NDEV), F32),
            pltpu.VMEM((8, NDEV), F32),
            pltpu.VMEM((4, 8, NDEV), F32),
            pltpu.VMEM((8, NDEV), F32),
            pltpu.VMEM((3, 8, NDEV), F32),
            pltpu.VMEM((2, NDEV), F32),
            pltpu.VMEM((2 * NDEV, NDEV), F32),
            dma((CASES,)),
            dma,
            dma,
            dma((6,)),
            dma((7,)),
            dma((7,)),
            dma((6,)),
            dma((6,)),
        ],
        compiler_params=pltpu.CompilerParams(
            collective_id=1, has_side_effects=True, vmem_limit_bytes=48 * 1024 * 1024
        ),
    )(
        displacement,
        load,
        home_slot.reshape(1, NDEV),
        state_slot.reshape(1, NDEV),
        phase_moduli,
        micro_state.reshape(ROWS, NDEV),
        phases,
        jnp.asarray(floats),
        jnp.asarray(ints),
    )
    return new_state.reshape(CASES, 3, VOX, NDEV), displaced, residual, norm[0, 0]


def solution(mesh):
    both = ("sub", "rve")
    return jax.shard_map(
        per_device,
        mesh=mesh,
        in_specs=(
            P(None, "sub", "rve", None),
            P(None, "sub", "rve", None),
            P(both),
            P(None, None, None, both),
            P(both),
            P(None, both),
            P(),
        ),
        out_specs=(
            P(None, None, None, both),
            P(None, "sub", "rve", None),
            P(None, "sub", "rve", None),
            P(),
        ),
        check_vma=False,
    )
```

profile of v0, /device:TPU:1, one launch (start us, length us, event | category | flops | bytes accessed | tf_op | source)
XLA Modules:
  0.0 75.9 jit_solution(14870967710714080098)
XLA Ops:
  0.6 0.0 copy-start
  0.6 1.6 %copy-done = f32[7,3,216,128]{3,2,1,0:T(8,128)S(1)} copy-done((f32[7,3,216,128]{3,2,1,0:T(8,128)S(1)}, f32[7,3,216,128]{3,2,1,0:T(8,128)}, u32[]{:S(2)}) %copy-start) | copy-done | bytes 2322456
  2.3 0.0 copy-start.1
  2.3 0.9 %copy-done.1 = s32[216,128]{1,0:T(8,128)S(1)} copy-done((s32[216,128]{1,0:T(8,128)S(1)}, s32[216,128]{1,0:T(8,128)}, u32[]{:S(2)}) %copy-start.1) | copy-done | bytes 110616
  3.2 0.0 copy-start.2
  3.2 0.7 copy-done.2
  3.9 0.0 copy-start.3
  3.9 0.7 copy-done.3
  4.6 0.0 copy-start.4
  4.6 0.7 copy-done.4
  5.3 0.0 copy-start.5
  5.3 0.7 copy-done.5
  6.0 0.0 copy-start.6
  6.0 0.7 copy-done.6
  6.7 0.0 copy-start.7
  6.7 0.7 copy-done.7
  7.3 0.0 copy-start.8
  7.3 0.7 copy-done.8
  8.0 63.6 %shard_map.120 = (f32[4536,128]{1,0:T(8,128)S(1)}, f32[3,1,2,8]{3,2,1,0:T(2,128)S(1)}, f32[3,1,2,8]{3,2,1,0:T(2,128)S(1)}, f32[1,1]{1,0:T(1,128)}) custom-call(f32[3,1,2,8]{3,2,1,0:T(2,128)S(1)} %copy-done.4, f32[3,1,2,8]{3,2,1,0:T(2,128)S(1)} %copy-done.5, s32[1,128]{1,0:T(1,128)S(1)} %bitcast.7, s32[1,128]{1,0:T(1,128)S(1)} %bitcast.8, ...), custom_call_target="tpu_custom_call" | custom-call | tf_op jit(solution)/shard_map/pallas_call | solution.py:545
  71.6 1.4 %copy.17 = f32[7,3,216,128]{3,2,1,0:T(8,128)} copy(f32[7,3,216,128]{3,2,1,0:T(8,128)S(1)} %bitcast.6) | data formatting | bytes 4644864
  73.0 0.6 copy.18
  73.6 0.6 copy.19
Async XLA Ops:
  0.6 1.7 %copy-start = (f32[7,3,216,128]{3,2,1,0:T(8,128)S(1)}, f32[7,3,216,128]{3,2,1,0:T(8,128)}, u32[]{:S(2)}) copy-start(f32[7,3,216,128]{3,2,1,0:T(8,128)} %param.12) | copy-start | bytes 6967300
  2.3 0.9 %copy-start.1 = (s32[216,128]{1,0:T(8,128)S(1)}, s32[216,128]{1,0:T(8,128)}, u32[]{:S(2)}) copy-start(s32[216,128]{1,0:T(8,128)} %phase_ref.1) | copy-start | bytes 331780
  3.2 0.7 copy-start.2
  3.9 0.7 copy-start.3
  4.6 0.7 copy-start.4
  5.3 0.7 copy-start.5
  6.0 0.7 copy-start.6
  6.7 0.7 copy-start.7
  7.3 0.7 copy-start.8
where the time goes:
time: 76.3 us; the launch traced here: 75.9 us
  Pallas kernels  63.6 us (83%)
  local copies, waits for them, and re-layouts  9.86 us (13%)
  between operations  2.41 us (3%)
    pallas_call x1, Pallas kernels, per_device(): pl.pallas_call(kernel, out_shape=(jax.ShapeDtypeStruct((ROWS, NDEV), F32)...  63.6 us
    unnamed x21, local copies, waits for them, and re-layouts  9.86 us

commit v1 on v0

--- a/solution.py
+++ b/solution.py
@@ -19,11 +19,12 @@
 NSUB = 32
 ROWS = CASES * 3 * VOX
 CASE_ROWS = 3 * VOX
-CHUNKS = (8, 8, 8, 8, 4)
-FIRST = (0, 8, 16, 24, 32)
-CHUNK_AT = {0: 0, 1: 1, 3: 2, 4: 3, 6: 4}
+CHUNKS = (6, 5, 5, 5, 5, 5, 5)
+FIRST = (0, 6, 11, 16, 21, 26, 31)
+LAST = len(CHUNKS) - 1
+RETURN, NORM = LAST + 1, LAST + 2
 CELLS = 36
-MESH = pl.DeviceIdType.MESH
+LOGICAL = pl.DeviceIdType.LOGICAL
 F32 = jnp.float32
 TERMS = (((0, 0), (2, 4), (1, 5)), ((1, 1), (2, 3), (0, 5)), ((2, 2), (1, 3), (0, 4)))
 
@@ -63,8 +64,12 @@
     return floats, ints
 
 
-def dev(d):
-    return (d // NRVE, lax.rem(d, NRVE))
+def around(step):
+    return min(step, 4 - step)
+
+
+SPREAD = [((i // 16 + i) % 4, (i // 4 + i) % 4, c, i % 4) for c in range(2) for i in range(64)][1:]
+FARTHEST = sorted(SPREAD, key=lambda o: -(around(o[0]) + around(o[1]) + around(o[3]) + 0.3 * o[2]))
 
 
 def lanes(x, index):
@@ -87,22 +92,40 @@
 
 
 def kernel(
-    disp_ref, load_ref, home_ref, state_slot_ref, moduli_ref, micro_ref, phase_ref, float_ref, int_ref,
+    disp_hbm, load_hbm, home_hbm, state_hbm, moduli_hbm, float_hbm, int_hbm, micro_ref, phase_ref,
     new_ref, displaced_ref, residual_ref, norm_ref,
-    xin, ph, send0, send1, send2, send3, send4, recv0, recv1, recv2, recv3, recv4,
-    nat, outb, lam, mu, w, p0, p1, ap, sig, sums, av, ret_out, ret_in, dtile, dhalo, ntile, nhalo, nrow, nall,
-    in_sem, ph_sem, out_sem, local_sem, send_sem, recv_sem, near_send, near_recv,
+    disp_ref, load_ref, home_ref, state_slot_ref, moduli_ref, float_ref, int_ref, xin, ph, send0, send1, send2, send3, send4, send5, send6, recv0, recv1, recv2, recv3, recv4, recv5, recv6,
+    nat, lam, mu, w, p0, p1, ap, sig, keep, av, ret_out, ret_in, dtile, dhalo, ntile, nhalo, nrow, nall,
+    small_sem, in_sem, ph_sem, local_sem, send_sem, recv_sem, near_send, near_recv,
 ):
     sub, rve = lax.axis_index("sub"), lax.axis_index("rve")
     me = sub * NRVE + rve
-    sends = (send0, send1, send2, send3, send4)
-    recvs = (recv0, recv1, recv2, recv3, recv4)
+    sends = (send0, send1, send2, send3, send4, send5, send6)
+    recvs = (recv0, recv1, recv2, recv3, recv4, recv5, recv6)
+    along_z = [lax.rem(sub // 8 + i, 4) * 32 for i in range(4)]
+    along_y = [lax.rem(lax.rem(sub // 2, 4) + i, 4) * 8 for i in range(4)]
+    along_c = [lax.rem(lax.rem(sub, 2) + i, 2) * 4 for i in range(2)]
+    along_x = [lax.rem(rve + i, 4) for i in range(4)]
+
+    def others(order):
+        for z, y, c, x in order:
+            yield along_z[z] + along_y[y] + (along_c[c] + along_x[x])
+
+    other = along_z[0] + along_y[0] + (along_c[0] + along_x[1])
 
     barrier = pltpu.get_barrier_semaphore()
 
-    @pl.loop(1, NDEV)
-    def _(k):
-        pl.semaphore_signal(barrier, inc=1, device_id=dev(lax.rem(me + k, NDEV)), device_id_type=MESH)
+    for d in others(FARTHEST):
+        pl.semaphore_signal(barrier, inc=1, device_id=d, device_id_type=LOGICAL)
+
+    small = []
+    pairs = (
+        (state_hbm, state_slot_ref), (home_hbm, home_ref), (disp_hbm, disp_ref), (load_hbm, load_ref),
+        (moduli_hbm, moduli_ref), (float_hbm, float_ref), (int_hbm, int_ref),
+    )
+    for i, (src, dst) in enumerate(pairs):
+        small.append(pltpu.make_async_copy(src, dst, small_sem.at[i]))
+        small[-1].start()
 
     loads = []
     for position in range(CASES):
@@ -117,6 +140,8 @@
     phase_load = pltpu.make_async_copy(phase_ref, ph.at[pl.ds(0, VOX)], ph_sem)
     phase_load.start()
 
+    for copy in small:
+        copy.wait()
     dtile[...] = jnp.zeros((8, NDEV), F32)
     for i in range(3):
         for y in range(2):
@@ -139,30 +164,21 @@
         sends[chunk][pl.ds(row, NDEV, stride=pitch), :] = jnp.concatenate(parts, axis=0).T
 
     def prepare_chunk(chunk):
-        rows = CHUNKS[chunk]
-        if chunk < 4:
-            for row in range(rows):
-                prepare(chunk, row, False)
-        else:
-            for row in range(rows):
-                prepare(chunk, row, row == rows - 1)
+        for row in range(CHUNKS[chunk]):
+            prepare(chunk, row, FIRST[chunk] + row == 35)
 
     def send_chunk(chunk):
         rows = CHUNKS[chunk]
-        own = pl.ds(pl.multiple_of(me * rows, rows), rows)
-
-        @pl.loop(1, NDEV)
-        def _(k):
-            d = lax.rem(me + k, NDEV)
+        own = pl.ds(me * rows, rows)
+        for d in others(SPREAD):
             pltpu.make_async_remote_copy(
-                src_ref=sends[chunk].at[pl.ds(pl.multiple_of(d * rows, rows), rows)],
+                src_ref=sends[chunk].at[pl.ds(d * rows, rows)],
                 dst_ref=recvs[chunk].at[own],
                 send_sem=send_sem.at[chunk],
                 recv_sem=recv_sem.at[chunk],
-                device_id=dev(d),
-                device_id_type=MESH,
+                device_id=d,
+                device_id_type=LOGICAL,
             ).start()
-
         pltpu.make_async_copy(sends[chunk].at[own], recvs[chunk].at[own], local_sem.at[chunk]).start()
 
     def whole(src, dst, rows, index):
@@ -171,8 +187,8 @@
             dst_ref=dst.at[pl.ds(0, (NDEV - 1) * rows)],
             send_sem=send_sem.at[index],
             recv_sem=recv_sem.at[index],
-            device_id=dev(lax.rem(me + 1, NDEV)),
-            device_id_type=MESH,
+            device_id=other,
+            device_id_type=LOGICAL,
         )
 
     for position in (0, 1):
@@ -189,8 +205,8 @@
             dst_ref=dst,
             send_sem=near_send.at[index],
             recv_sem=near_recv.at[index],
-            device_id=(to_sub, to_rve),
-            device_id_type=MESH,
+            device_id=to_sub * NRVE + to_rve,
+            device_id_type=LOGICAL,
         )
 
     steps = ((0, 1), (1, 0), (1, 1))
@@ -198,17 +214,11 @@
     for copy in halo_in:
         copy.start()
     send_chunk(0)
-    for position in (2, 3):
-        loads[position].wait()
-    prepare_chunk(1)
-    send_chunk(1)
-    loads[4].wait()
-    prepare_chunk(2)
-    send_chunk(2)
-    for position in (5, 6):
-        loads[position].wait()
-    prepare_chunk(3)
-    send_chunk(3)
+    for chunk in range(1, LAST):
+        if chunk + 1 < CASES:
+            loads[chunk + 1].wait()
+        prepare_chunk(chunk)
+        send_chunk(chunk)
 
     for copy in halo_in:
         copy.wait()
@@ -233,12 +243,15 @@
     for m in range(6):
         strain_rows = jnp.where(row8 == m, spread(strains[m]), strain_rows)
     xin[pl.ds(ROWS, 8), :] = strain_rows
-    prepare_chunk(4)
-    send_chunk(4)
+    prepare_chunk(LAST)
+    send_chunk(LAST)
 
     phase_load.wait()
     ph[pl.ds(VOX, 8), :] = jnp.zeros((8, NDEV), jnp.int32)
     inside = row8 < R
+    moduli = [
+        [jnp.broadcast_to(moduli_ref[which : which + 1, p : p + 1], (8, NDEV)) for p in range(3)] for which in range(2)
+    ]
 
     @pl.loop(0, CELLS)
     def _(cell):
@@ -246,8 +259,8 @@
         for which, out in ((0, lam), (1, mu)):
             value = jnp.where(
                 label == 0,
-                moduli_ref[which, 0],
-                jnp.where(label == 1, moduli_ref[which, 1], moduli_ref[which, 2]),
+                moduli[which][0],
+                jnp.where(label == 1, moduli[which][1], moduli[which][2]),
             )
             out[cell] = jnp.where(inside, value, 0.0)
 
@@ -257,7 +270,7 @@
 
     def receive(chunk):
         rows = CHUNKS[chunk]
-        own = pl.ds(pl.multiple_of(me * rows, rows), rows)
+        own = pl.ds(me * rows, rows)
         whole(sends[chunk], recvs[chunk], rows, chunk).wait_recv()
         pltpu.make_async_copy(sends[chunk].at[own], recvs[chunk].at[own], local_sem.at[chunk]).wait()
         for row in range(rows):
@@ -318,10 +331,22 @@
     def across(x):
         return spread(jnp.sum(x, axis=0, keepdims=True))
 
+    def finish(case):
+        alpha0, alpha1 = keep[0], keep[1]
+
+        @pl.loop(0, R)
+        def _(a):
+            for i in range(3):
+                to = case * CASE_ROWS + i * VOX + a * (R * R)
+                for b in range(R):
+                    at = i * CELLS + a * R + b
+                    value = w[at] + alpha0 * p0[at] + alpha1 * p1[at]
+                    new_ref[pl.ds(to + b * R, R), :] = value[0:R, :]
+
     def case_body(position, carry):
-        for when, chunk in CHUNK_AT.items():
-
-            @pl.when(position == when)
+        for chunk in range(CASES):
+
+            @pl.when(position == chunk)
             def _():
                 receive(chunk)
 
@@ -332,11 +357,12 @@
             unit = jnp.where(position == m, 1.0, 0.0).astype(F32)
             applied.append(jnp.where(position == CASES - 1, spread(macro[m : m + 1, :]), unit))
 
-        @pl.loop(0, CELLS)
-        def _(cell):
+        @pl.loop(0, R)
+        def _(a):
             for i in range(3):
-                at = position * CASE_ROWS + i * VOX + cell * R
-                w[i * CELLS + cell] = jnp.where(inside, nat[pl.ds(at, 8), :], 0.0)
+                at = position * CASE_ROWS + i * VOX + a * (R * R)
+                for b in range(R):
+                    w[i * CELLS + a * R + b] = jnp.where(inside, nat[pl.ds(at + b * R, 8), :], 0.0)
 
         total0 = stresses(w, applied)
 
@@ -346,7 +372,8 @@
                 for i in range(3):
                     value = -force[i]
                     p0[i * CELLS + a * R + b] = value
-                    rr = rr + value * value
+                    force[i] = value * value
+                rr = rr + (force[0] + (force[1] + force[2]))
             return rr
 
         rr = across(lax.fori_loop(0, R, first, zero))
@@ -357,20 +384,23 @@
                 force = force_at(p0, a, b)
                 for i in range(3):
                     ap[i * CELLS + a * R + b] = force[i]
-                    curve = curve + p0[i * CELLS + a * R + b] * force[i]
+                    force[i] = p0[i * CELLS + a * R + b] * force[i]
+                curve = curve + (force[0] + (force[1] + force[2]))
             return curve
 
         alpha0 = rr / across(lax.fori_loop(0, R, second, zero))
 
         def reduce(a, total):
+            total = list(total)
             for j in range(3 * R):
                 at = a * (3 * R) + j
                 value = p0[at] - alpha0 * ap[at]
                 p1[at] = value
-                total = total + value * value
-            return total
-
-        rn = across(lax.fori_loop(0, R, reduce, zero))
+                total[j % 6] = total[j % 6] + value * value
+            return tuple(total)
+
+        parts = lax.fori_loop(0, R, reduce, (zero,) * 6)
+        rn = across(((parts[0] + parts[1]) + (parts[2] + parts[3])) + (parts[4] + parts[5]))
         beta = rn / rr
 
         @pl.loop(0, R)
@@ -385,10 +415,10 @@
                 stress, eps = stress_at(p1, a, b, None)
                 for m in range(6):
                     total[m] = total[m] + stress[m]
-                    curve = curve + stress[m] * eps[m]
-                for i in range(3):
-                    here = p1[i * CELLS + a * R + b]
-                    curve = curve + (STAB * here) * here
+                work = [stress[m] * eps[m] for m in range(6)]
+                here = [p1[i * CELLS + a * R + b] for i in range(3)]
+                kept = STAB * ((here[0] * here[0] + here[1] * here[1]) + here[2] * here[2])
+                curve = curve + (((work[0] + work[1]) + (work[2] + work[3])) + ((work[4] + work[5]) + kept))
             return (curve, *total)
 
         found = lax.fori_loop(0, R, third, (zero,) * 7)
@@ -397,46 +427,40 @@
             mean = jnp.sum(total0[m] + alpha0 * total1[m] + alpha1 * found[1 + m], axis=0, keepdims=True)
             av[pl.ds(case * 6 + m, 1), :] = mean * (1.0 / VOX)
 
-        @pl.loop(0, CELLS)
-        def _(cell):
-            for i in range(3):
-                at = i * CELLS + cell
-                value = w[at] + alpha0 * p0[at] + alpha1 * p1[at]
-                outb[pl.ds(case * CASE_ROWS + i * VOX + cell * R, R), :] = value[0:R, :]
-
-        span = pl.ds(pl.multiple_of(case * CASE_ROWS, 8), CASE_ROWS)
-        pltpu.make_async_copy(outb.at[span], new_ref.at[span], out_sem).start()
+        keep[0], keep[1] = alpha0, alpha1
+
+        @pl.when(position < LAST)
+        def _():
+            finish(case)
+
         return carry
 
     lax.fori_loop(0, CASES, case_body, 0)
 
     def send_rows(src, dst, rows, index):
         own = pl.ds(me * rows, rows)
-
-        @pl.loop(1, NDEV)
-        def _(k):
-            d = lax.rem(me + k, NDEV)
+        for d in others(FARTHEST):
             pltpu.make_async_remote_copy(
-                src_ref=src.at[pl.ds(d * rows, rows)] if index == 5 else src,
+                src_ref=src.at[pl.ds(d, 1)] if index == RETURN else src,
                 dst_ref=dst.at[own],
                 send_sem=send_sem.at[index],
                 recv_sem=recv_sem.at[index],
-                device_id=dev(d),
-                device_id_type=MESH,
+                device_id=d,
+                device_id_type=LOGICAL,
             ).start()
 
     ret_out[...] = av[...].T
-    send_rows(ret_out, ret_in, 1, 5)
+    send_rows(ret_out, ret_in, 1, RETURN)
     own_row = pl.ds(me, 1)
-    own_copy = pltpu.make_async_copy(ret_out.at[own_row], ret_in.at[own_row], local_sem.at[5])
+    own_copy = pltpu.make_async_copy(ret_out.at[own_row], ret_in.at[own_row], local_sem.at[RETURN])
     own_copy.start()
-    load_rows = zero
+    finish(0)
     for i in range(3):
         for y in range(2):
             dhalo[3, i : i + 1, 8 * y : 8 * y + 8] = load_ref[i, 0, y : y + 1, :]
     load_rows = jnp.where((lane < 16) & (row8 < 3), dhalo[3], 0.0)
     load_square = jnp.sum(load_rows * load_rows, keepdims=True)
-    whole(ret_out, ret_in, 1, 5).wait_recv()
+    whole(ret_out, ret_in, 1, RETURN).wait_recv()
     own_copy.wait()
     back = ret_in[...].T
     home_rows = spread(home_dev)
@@ -476,7 +500,7 @@
     halo_out = [near(3 + i, ntile, nhalo.at[i], s, r) for i, (s, r) in enumerate(steps)]
     for copy in halo_out:
         copy.start()
-    send_rows(nrow, nall, 2, 6)
+    send_rows(nrow, nall, 2, NORM)
 
     for copy in halo_out:
         copy.wait()
@@ -495,10 +519,10 @@
     pltpu.make_async_remote_copy(
         src_ref=nall.at[pl.ds(0, 2 * NDEV - 2)],
         dst_ref=nall.at[pl.ds(0, 2 * NDEV - 2)],
-        send_sem=send_sem.at[6],
-        recv_sem=recv_sem.at[6],
-        device_id=dev(lax.rem(me + 1, NDEV)),
-        device_id_type=MESH,
+        send_sem=send_sem.at[NORM],
+        recv_sem=recv_sem.at[NORM],
+        device_id=other,
+        device_id_type=LOGICAL,
     ).wait_recv()
     turn = jnp.where(lax.rem(row8, 4) == 0, row8 + 3, row8 - 1)
     square = zero
@@ -520,45 +544,60 @@
             square = square + value * value
     norm_ref[...] = jnp.sqrt(jnp.sum(square, keepdims=True) / jnp.sum(load_sum, keepdims=True))
 
-    for chunk in range(5):
+    for chunk in range(CASES):
         whole(sends[chunk], recvs[chunk], CHUNKS[chunk], chunk).wait_send()
-    whole(ret_out, ret_in, 1, 5).wait_send()
+    whole(ret_out, ret_in, 1, RETURN).wait_send()
     pltpu.make_async_remote_copy(
         src_ref=nall.at[pl.ds(0, 2 * NDEV - 2)],
         dst_ref=nall.at[pl.ds(0, 2 * NDEV - 2)],
-        send_sem=send_sem.at[6],
-        recv_sem=recv_sem.at[6],
-        device_id=dev(lax.rem(me + 1, NDEV)),
-        device_id_type=MESH,
+        send_sem=send_sem.at[NORM],
+        recv_sem=recv_sem.at[NORM],
+        device_id=other,
+        device_id_type=LOGICAL,
     ).wait_send()
-    pltpu.make_async_copy(outb, new_ref, out_sem).wait()
 
 
 def per_device(displacement, load, home_slot, micro_state, state_slot, phases, phase_moduli):
     floats, ints = tables()
     vmem = pl.BlockSpec(memory_space=pltpu.VMEM)
-    smem = pl.BlockSpec(memory_space=pltpu.SMEM)
-    hbm = pl.BlockSpec(memory_space=pl.ANY)
+    hbm = pl.BlockSpec(memory_space=pltpu.HBM)
     buffers = [pltpu.VMEM((NDEV * rows, NDEV), F32) for rows in CHUNKS]
     cells = pltpu.VMEM((3 * CELLS, 8, NDEV), F32)
     dma = pltpu.SemaphoreType.DMA
+    arguments = (
+        displacement,
+        load,
+        home_slot.reshape(1, NDEV),
+        state_slot.reshape(1, NDEV),
+        phase_moduli,
+        jnp.asarray(floats),
+        jnp.asarray(ints),
+        micro_state.reshape(ROWS, NDEV),
+        phases,
+    )
     new_state, displaced, residual, norm = pl.pallas_call(
         kernel,
         out_shape=(
-            jax.ShapeDtypeStruct((ROWS, NDEV), F32),
-            jax.ShapeDtypeStruct(displacement.shape, F32),
-            jax.ShapeDtypeStruct(displacement.shape, F32),
+            pltpu.VMEM((ROWS, NDEV), F32),
+            pltpu.VMEM(displacement.shape, F32),
+            pltpu.VMEM(displacement.shape, F32),
             jax.ShapeDtypeStruct((1, 1), F32),
         ),
-        in_specs=[vmem, vmem, vmem, vmem, smem, hbm, hbm, vmem, vmem],
-        out_specs=(hbm, vmem, vmem, vmem),
+        in_specs=[hbm] * 9,
+        out_specs=(vmem,) * 4,
         scratch_shapes=[
+            pltpu.VMEM(displacement.shape, F32),
+            pltpu.VMEM(load.shape, F32),
+            pltpu.VMEM((1, NDEV), jnp.int32),
+            pltpu.VMEM((1, NDEV), jnp.int32),
+            pltpu.VMEM(phase_moduli.shape, F32),
+            pltpu.VMEM(floats.shape, F32),
+            pltpu.VMEM(ints.shape, jnp.int32),
             pltpu.VMEM((ROWS + 72, NDEV), F32),
             pltpu.VMEM((VOX + 8, NDEV), jnp.int32),
             *buffers,
             *buffers,
             pltpu.VMEM((ROWS + 72, NDEV), F32),
-            pltpu.VMEM((ROWS, NDEV), F32),
             pltpu.VMEM((CELLS, 8, NDEV), F32),
             pltpu.VMEM((CELLS, 8, NDEV), F32),
             cells,
@@ -566,7 +605,7 @@
             cells,
             cells,
             pltpu.VMEM((6 * CELLS, 8, NDEV), F32),
-            pltpu.VMEM((12, 8, NDEV), F32),
+            pltpu.VMEM((2, 8, NDEV), F32),
             pltpu.VMEM((NDEV, NDEV), F32),
             pltpu.VMEM((NDEV, NDEV), F32),
             pltpu.VMEM((NDEV, NDEV), F32),
@@ -576,29 +615,19 @@
             pltpu.VMEM((3, 8, NDEV), F32),
             pltpu.VMEM((2, NDEV), F32),
             pltpu.VMEM((2 * NDEV, NDEV), F32),
+            dma((7,)),
             dma((CASES,)),
             dma,
-            dma,
-            dma((6,)),
-            dma((7,)),
-            dma((7,)),
+            dma((CASES + 1,)),
+            dma((CASES + 2,)),
+            dma((CASES + 2,)),
             dma((6,)),
             dma((6,)),
         ],
         compiler_params=pltpu.CompilerParams(
             collective_id=1, has_side_effects=True, vmem_limit_bytes=48 * 1024 * 1024
         ),
-    )(
-        displacement,
-        load,
-        home_slot.reshape(1, NDEV),
-        state_slot.reshape(1, NDEV),
-        phase_moduli,
-        micro_state.reshape(ROWS, NDEV),
-        phases,
-        jnp.asarray(floats),
-        jnp.asarray(ints),
-    )
+    )(*[pltpu.with_memory_space_constraint(x, pltpu.HBM) for x in arguments])
     return new_state.reshape(CASES, 3, VOX, NDEV), displaced, residual, norm[0, 0]
 
 

time: 76.3 us -> 59.2 us (0.78)
  Pallas kernels: 63.6 us -> 54.2 us
  local copies, waits for them, and re-layouts: 9.86 us -> 2.55 us
    pallas_call x1, Pallas kernels: 63.6 us -> 54.2 us  [per_device(): pl.pallas_call(kernel, out_shape=(pltpu.VMEM((ROWS, NDEV), F32), pltpu.VM...]
    unnamed x21 -> x3, local copies, waits for them, and re-layouts: 9.86 us -> 2.55 us
where the time goes in v1:
time: 59.2 us; the launch traced here: 59.1 us
  Pallas kernels  54.2 us (92%)
  local copies, waits for them, and re-layouts  2.55 us (4%)
  between operations  2.33 us (4%)
    pallas_call x1, Pallas kernels, per_device(): pl.pallas_call(kernel, out_shape=(pltpu.VMEM((ROWS, NDEV), F32), pltpu.VM...  54.2 us
    unnamed x3, local copies, waits for them, and re-layouts  2.55 us

profile of v1, /device:TPU:1, one launch (start us, length us, event | category | flops | bytes accessed | tf_op | source)
XLA Modules:
  0.0 59.1 jit_solution(11734217010165831010)
XLA Ops:
  0.6 54.2 %shard_map.120 = (f32[4536,128]{1,0:T(8,128)S(1)}, f32[3,1,2,8]{3,2,1,0:T(2,128)S(1)}, f32[3,1,2,8]{3,2,1,0:T(2,128)S(1)}, f32[1,1]{1,0:T(1,128)}) custom-call(f32[3,1,2,8]{3,2,1,0:T(2,128)} %disp_hbm.1, f32[3,1,2,8]{3,2,1,0:T(2,128)} %load_hbm.1, s32[1,128]{1,0:T(1,128)} %bitcast.7, s32[1,128]{1,0:T(1,128)} %bitcast.8, f32[2,3]{1,0:T(2,128)} %moduli_hbm.1, ...), custom_call_target="tpu_custom_call" | custom-call | tf_op jit(solution)/shard_map/pallas_call | solution.py:578
  54.8 1.4 %copy.17 = f32[7,3,216,128]{3,2,1,0:T(8,128)} copy(f32[7,3,216,128]{3,2,1,0:T(8,128)S(1)} %bitcast.5) | data formatting | bytes 4644864
  56.2 0.6 copy.18
  56.8 0.6 copy.19

commit v2 on v1

--- a/solution.py
+++ b/solution.py
@@ -22,6 +22,10 @@
 CHUNKS = (6, 5, 5, 5, 5, 5, 5)
 FIRST = (0, 6, 11, 16, 21, 26, 31)
 LAST = len(CHUNKS) - 1
+ORDER = (1, 2, 0, 3, 4, 5, 6)
+MACRO = 2
+STRAIN_ROW = 3 * CASE_ROWS
+STRESS_ROW = 7 * CASE_ROWS + 8
 RETURN, NORM = LAST + 1, LAST + 2
 CELLS = 36
 LOGICAL = pl.DeviceIdType.LOGICAL
@@ -64,6 +68,10 @@
     return floats, ints
 
 
+def base_of(position):
+    return position * CASE_ROWS + 8 * ((position + 3) // 6)
+
+
 def around(step):
     return min(step, 4 - step)
 
@@ -95,7 +103,7 @@
     disp_hbm, load_hbm, home_hbm, state_hbm, moduli_hbm, float_hbm, int_hbm, micro_ref, phase_ref,
     new_ref, displaced_ref, residual_ref, norm_ref,
     disp_ref, load_ref, home_ref, state_slot_ref, moduli_ref, float_ref, int_ref, xin, ph, send0, send1, send2, send3, send4, send5, send6, recv0, recv1, recv2, recv3, recv4, recv5, recv6,
-    nat, lam, mu, w, p0, p1, ap, sig, keep, av, ret_out, ret_in, dtile, dhalo, ntile, nhalo, nrow, nall,
+    nat, lam, mu, w, p0, p1, ap, sig, keep, av, ret_out, ret_in, dtile, dhalo, ntile, nhalo, nrow, nall, whole_residual,
     small_sem, in_sem, ph_sem, local_sem, send_sem, recv_sem, near_send, near_recv,
 ):
     sub, rve = lax.axis_index("sub"), lax.axis_index("rve")
@@ -128,11 +136,10 @@
         small[-1].start()
 
     loads = []
-    for position in range(CASES):
-        case = (position + 1) % CASES
+    for position, case in enumerate(ORDER):
         copy = pltpu.make_async_copy(
             micro_ref.at[pl.ds(case * CASE_ROWS, CASE_ROWS)],
-            xin.at[pl.ds(position * CASE_ROWS, CASE_ROWS)],
+            xin.at[pl.ds(base_of(position), CASE_ROWS)],
             in_sem.at[position],
         )
         copy.start()
@@ -151,21 +158,21 @@
     state_index = spread(inverse(lax.shift_right_logical(state_slot_ref[...], 7)))
     home_index = spread(inverse(home_dev))
 
-    def prepare(chunk, row, last):
-        base = pl.multiple_of((FIRST[chunk] + row) * NDEV, NDEV)
+    def prepare(chunk, row):
         parts = []
         for i in range(16):
-            if last and i > 7:
-                parts.append(jnp.zeros((8, NDEV), F32))
-            else:
-                block = xin[pl.ds(base + 8 * i, 8), :]
-                parts.append(lanes(block, home_index if last and i == 7 else state_index))
-        pitch = CHUNKS[chunk]
-        sends[chunk][pl.ds(row, NDEV, stride=pitch), :] = jnp.concatenate(parts, axis=0).T
+            at = (FIRST[chunk] + row) * NDEV + 8 * i
+            block = xin[pl.ds(at, 8), :]
+            if at == STRAIN_ROW:
+                block = lanes(block, home_index)
+            elif at != STRESS_ROW:
+                block = lanes(block, state_index)
+            parts.append(block)
+        sends[chunk][pl.ds(row, NDEV, stride=CHUNKS[chunk]), :] = jnp.concatenate(parts, axis=0).T
 
     def prepare_chunk(chunk):
         for row in range(CHUNKS[chunk]):
-            prepare(chunk, row, FIRST[chunk] + row == 35)
+            prepare(chunk, row)
 
     def send_chunk(chunk):
         rows = CHUNKS[chunk]
@@ -214,11 +221,9 @@
     for copy in halo_in:
         copy.start()
     send_chunk(0)
-    for chunk in range(1, LAST):
-        if chunk + 1 < CASES:
-            loads[chunk + 1].wait()
-        prepare_chunk(chunk)
-        send_chunk(chunk)
+    loads[2].wait()
+    prepare_chunk(1)
+    send_chunk(1)
 
     for copy in halo_in:
         copy.wait()
@@ -242,9 +247,12 @@
     strain_rows = jnp.zeros((8, NDEV), F32)
     for m in range(6):
         strain_rows = jnp.where(row8 == m, spread(strains[m]), strain_rows)
-    xin[pl.ds(ROWS, 8), :] = strain_rows
-    prepare_chunk(LAST)
-    send_chunk(LAST)
+    xin[pl.ds(STRAIN_ROW, 8), :] = strain_rows
+    for chunk in range(MACRO, LAST):
+        loads[chunk + 1].wait()
+        prepare_chunk(chunk)
+        send_chunk(chunk)
+    xin[pl.ds(STRESS_ROW + 8, 56), :] = jnp.zeros((56, NDEV), F32)
 
     phase_load.wait()
     ph[pl.ds(VOX, 8), :] = jnp.zeros((8, NDEV), jnp.int32)
@@ -343,6 +351,41 @@
                     value = w[at] + alpha0 * p0[at] + alpha1 * p1[at]
                     new_ref[pl.ds(to + b * R, R), :] = value[0:R, :]
 
+    for i in range(3):
+        for y in range(2):
+            dhalo[3, i : i + 1, 8 * y : 8 * y + 8] = load_ref[i, 0, y : y + 1, :]
+    home_rows = spread(home_dev)
+    grad = [float_ref[8 * k : 8 * k + 8, :] for k in range(3)]
+
+    def to_nodes(value):
+        for step in (1, 2, 4):
+            value = value + pltpu.roll(value, NDEV - step, axis=1)
+        value = lanes(value, int_ref[0:8, :]) * (float_ref[24:32, :] * 0.125)
+        return jnp.sum(value, axis=0, keepdims=True)
+
+    def tiled(rows):
+        tile = zero
+        for r, value in enumerate(rows):
+            tile = jnp.where(row8 == r, spread(value), tile)
+        return tile
+
+    def assemble_force():
+        stress = lanes(nat[pl.ds(STRESS_ROW, 8), :], home_rows)
+        rows = []
+        for i in range(3):
+            value = zero
+            for k, m in TERMS[i]:
+                value = value + grad[k] * spread(stress[m : m + 1, :])
+            rows.append(to_nodes(value))
+        load_rows = jnp.where((lane < 16) & (row8 < 3), dhalo[3], 0.0)
+        load_square = jnp.sum(load_rows * load_rows, keepdims=True)
+        part = load_rows - tiled(rows)
+        first_row = part[0:1] + pltpu.roll(part[1:2], 64, axis=1)
+        second_row = jnp.where(lane[0:1] == NDEV - 1, jnp.broadcast_to(load_square, (1, NDEV)), part[2:3])
+        both = jnp.concatenate([first_row, second_row], axis=0)
+        nrow[...] = both
+        nall[pl.ds(me * 2, 2), :] = both
+
     def case_body(position, carry):
         for chunk in range(CASES):
 
@@ -350,17 +393,18 @@
             def _():
                 receive(chunk)
 
-        case = lax.rem(position + 1, CASES)
-        macro = nat[pl.ds(ROWS, 8), :]
+        plain = (position + 3) // 6
+        case = plain * position + (1 - plain) * lax.rem(position + 1, 3)
+        macro = nat[pl.ds(STRAIN_ROW, 8), :]
         applied = []
         for m in range(6):
-            unit = jnp.where(position == m, 1.0, 0.0).astype(F32)
-            applied.append(jnp.where(position == CASES - 1, spread(macro[m : m + 1, :]), unit))
+            unit = jnp.where(case == m + 1, 1.0, 0.0).astype(F32)
+            applied.append(jnp.where(position == MACRO, spread(macro[m : m + 1, :]), unit))
 
         @pl.loop(0, R)
         def _(a):
             for i in range(3):
-                at = position * CASE_ROWS + i * VOX + a * (R * R)
+                at = base_of(position) + i * VOX + a * (R * R)
                 for b in range(R):
                     w[i * CELLS + a * R + b] = jnp.where(inside, nat[pl.ds(at + b * R, 8), :], 0.0)
 
@@ -433,6 +477,12 @@
         def _():
             finish(case)
 
+        @pl.when(position == MACRO)
+        def _():
+            xin[pl.ds(STRESS_ROW, 8), :] = av[0:8, :]
+            prepare_chunk(LAST)
+            send_chunk(LAST)
+
         return carry
 
     lax.fori_loop(0, CASES, case_body, 0)
@@ -454,67 +504,32 @@
     own_row = pl.ds(me, 1)
     own_copy = pltpu.make_async_copy(ret_out.at[own_row], ret_in.at[own_row], local_sem.at[RETURN])
     own_copy.start()
-    finish(0)
-    for i in range(3):
-        for y in range(2):
-            dhalo[3, i : i + 1, 8 * y : 8 * y + 8] = load_ref[i, 0, y : y + 1, :]
-    load_rows = jnp.where((lane < 16) & (row8 < 3), dhalo[3], 0.0)
-    load_square = jnp.sum(load_rows * load_rows, keepdims=True)
+    assemble_force()
+    send_rows(nrow, nall, 2, NORM)
+    finish(ORDER[LAST])
     whole(ret_out, ret_in, 1, RETURN).wait_recv()
     own_copy.wait()
     back = ret_in[...].T
-    home_rows = spread(home_dev)
     at_home = [lanes(back[8 * i : 8 * i + 8, :], home_rows) for i in range(6)]
 
-    def averaged(case, m):
-        row = case * 6 + m
+    def tangent(m, j):
+        row = (1 + j) * 6 + m
         return at_home[row // 8][row % 8 : row % 8 + 1, :]
 
-    grad = [float_ref[8 * k : 8 * k + 8, :] for k in range(3)]
-    pick, mask = int_ref[0:8, :], float_ref[24:32, :]
-    node_rows = []
-    for kind in range(2):
-        for i in range(3):
-            value = zero
-            for k, m in TERMS[i]:
-                if kind == 0:
-                    inner = spread(averaged(0, m))
-                else:
-                    inner = zero
-                    for l, j in TERMS[i]:
-                        inner = inner + grad[l] * averaged(1 + j, m)
-                value = value + grad[k] * inner
-            for step in (1, 2, 4):
-                value = value + pltpu.roll(value, NDEV - step, axis=1)
-            value = lanes(value, pick) * (mask * 0.125)
-            node_rows.append(jnp.sum(value, axis=0, keepdims=True))
-    tile = zero
-    for r, value in enumerate(node_rows):
-        tile = jnp.where(row8 == r, spread(value), tile)
+    diagonal = []
+    for i in range(3):
+        value = zero
+        for k, m in TERMS[i]:
+            inner = zero
+            for l, j in TERMS[i]:
+                inner = inner + grad[l] * tangent(m, j)
+            value = value + grad[k] * inner
+        diagonal.append(to_nodes(value))
+    tile = tiled(diagonal)
     ntile[...] = tile
-    part = load_rows - jnp.where(row8 < 3, tile, 0.0)
-    first_row = part[0:1] + pltpu.roll(part[1:2], 64, axis=1)
-    second_row = jnp.where(lane[0:1] == NDEV - 1, jnp.broadcast_to(load_square, (1, NDEV)), part[2:3])
-    nrow[...] = jnp.concatenate([first_row, second_row], axis=0)
-    nall[pl.ds(me * 2, 2), :] = jnp.concatenate([first_row, second_row], axis=0)
     halo_out = [near(3 + i, ntile, nhalo.at[i], s, r) for i, (s, r) in enumerate(steps)]
     for copy in halo_out:
         copy.start()
-    send_rows(nrow, nall, 2, NORM)
-
-    for copy in halo_out:
-        copy.wait()
-    above = jnp.where(sub > 0, 1.0, 0.0).astype(F32)
-    node = jnp.where(lane < 16, tile, 0.0)
-    node = node + jnp.where(lane < 8, pltpu.roll(nhalo[0], NDEV - 16, axis=1), 0.0)
-    node = node + jnp.where(lane < 16, pltpu.roll(nhalo[1], NDEV - 24, axis=1) * above, 0.0)
-    node = node + jnp.where(lane < 8, pltpu.roll(nhalo[2], NDEV - 40, axis=1) * above, 0.0)
-    residual = load_rows[0:3] - node[0:3]
-    moved = dtile[0:3, :] + residual / jnp.maximum(node[3:6], FLOOR)
-    for i in range(3):
-        for y in range(2):
-            displaced_ref[i, 0, y : y + 1, :] = moved[i : i + 1, 8 * y : 8 * y + 8]
-            residual_ref[i, 0, y : y + 1, :] = residual[i : i + 1, 8 * y : 8 * y + 8]
 
     pltpu.make_async_remote_copy(
         src_ref=nall.at[pl.ds(0, 2 * NDEV - 2)],
@@ -541,8 +556,25 @@
             shifted = jnp.where(row8 < 4, pltpu.roll(before_z, 4, axis=0), pltpu.roll(plane, 4, axis=0))
             before_z = plane
             value = jnp.where(low < 16, value + shifted, 0.0)
+            whole_residual[half, pl.ds(block * 8, 8), :] = value
             square = square + value * value
-    norm_ref[...] = jnp.sqrt(jnp.sum(square, keepdims=True) / jnp.sum(load_sum, keepdims=True))
+    ratio = jnp.sqrt(jnp.sum(square, keepdims=True) / jnp.sum(load_sum, keepdims=True))
+    norm_ref[...] = jnp.broadcast_to(ratio, (8, NDEV))
+
+    for copy in halo_out:
+        copy.wait()
+    above = jnp.where(sub > 0, 1.0, 0.0).astype(F32)
+    node = jnp.where(lane < 16, tile, 0.0)
+    node = node + jnp.where(lane < 8, pltpu.roll(nhalo[0], NDEV - 16, axis=1), 0.0)
+    node = node + jnp.where(lane < 16, pltpu.roll(nhalo[1], NDEV - 24, axis=1) * above, 0.0)
+    node = node + jnp.where(lane < 8, pltpu.roll(nhalo[2], NDEV - 40, axis=1) * above, 0.0)
+    pair = whole_residual[0, pl.ds(me, 1), :]
+    residual = jnp.concatenate([pair, pltpu.roll(pair, 64, axis=1), whole_residual[1, pl.ds(me, 1), :]], axis=0)
+    moved = dtile[0:3, :] + residual / jnp.maximum(node[0:3], FLOOR)
+    for i in range(3):
+        for y in range(2):
+            displaced_ref[i, 0, y : y + 1, :] = moved[i : i + 1, 8 * y : 8 * y + 8]
+            residual_ref[i, 0, y : y + 1, :] = residual[i : i + 1, 8 * y : 8 * y + 8]
 
     for chunk in range(CASES):
         whole(sends[chunk], recvs[chunk], CHUNKS[chunk], chunk).wait_send()
@@ -555,6 +587,19 @@
         device_id=other,
         device_id_type=LOGICAL,
     ).wait_send()
+
+
+def write_out(new_vmem, displaced_vmem, residual_vmem, norm_vmem, new_ref, displaced_ref, residual_ref, norm_ref, sem):
+    copies = []
+    for case in range(CASES):
+        span = pl.ds(case * CASE_ROWS, CASE_ROWS)
+        copies.append((new_vmem.at[span], new_ref.at[span]))
+    copies += [(displaced_vmem, displaced_ref), (residual_vmem, residual_ref), (norm_vmem.at[pl.ds(0, 1)], norm_ref)]
+    copies = [pltpu.make_async_copy(src, dst, sem.at[i]) for i, (src, dst) in enumerate(copies)]
+    for copy in copies:
+        copy.start()
+    for copy in copies:
+        copy.wait()
 
 
 def per_device(displacement, load, home_slot, micro_state, state_slot, phases, phase_moduli):
@@ -575,13 +620,13 @@
         micro_state.reshape(ROWS, NDEV),
         phases,
     )
-    new_state, displaced, residual, norm = pl.pallas_call(
+    results = pl.pallas_call(
         kernel,
         out_shape=(
             pltpu.VMEM((ROWS, NDEV), F32),
             pltpu.VMEM(displacement.shape, F32),
             pltpu.VMEM(displacement.shape, F32),
-            jax.ShapeDtypeStruct((1, 1), F32),
+            pltpu.VMEM((8, NDEV), F32),
         ),
         in_specs=[hbm] * 9,
         out_specs=(vmem,) * 4,
@@ -615,6 +660,7 @@
             pltpu.VMEM((3, 8, NDEV), F32),
             pltpu.VMEM((2, NDEV), F32),
             pltpu.VMEM((2 * NDEV, NDEV), F32),
+            pltpu.VMEM((2, NDEV, NDEV), F32),
             dma((7,)),
             dma((CASES,)),
             dma,
@@ -628,6 +674,14 @@
             collective_id=1, has_side_effects=True, vmem_limit_bytes=48 * 1024 * 1024
         ),
     )(*[pltpu.with_memory_space_constraint(x, pltpu.HBM) for x in arguments])
+    new_state, displaced, residual, norm = pl.pallas_call(
+        write_out,
+        out_shape=tuple(pltpu.HBM(shape, F32) for shape in (results[0].shape, *[displacement.shape] * 2, (1, NDEV))),
+        in_specs=[vmem] * 4,
+        out_specs=(hbm,) * 4,
+        scratch_shapes=[dma((CASES + 3,))],
+        compiler_params=pltpu.CompilerParams(vmem_limit_bytes=4 * 1024 * 1024),
+    )(*results)
     return new_state.reshape(CASES, 3, VOX, NDEV), displaced, residual, norm[0, 0]
 
 

time: 59.2 us -> 53.5 us (0.904)
  local copies, waits for them, and re-layouts: 2.55 us -> 0 us
  between operations: 2.33 us -> 0.64 us
  Pallas kernels: 54.2 us -> 52.7 us
    pallas_call x1, Pallas kernels: 54.2 us -> 51.2 us  [per_device(): pl.pallas_call(kernel, out_shape=(pltpu.VMEM((ROWS, NDEV), F32), pltpu.VM...]
    unnamed x3 -> x0, local copies, waits for them, and re-layouts: 2.55 us -> none
    pallas_call x0 -> x1, Pallas kernels: none -> 1.48 us  [per_device(): pl.pallas_call(write_out, out_shape=tuple((pltpu.HBM(shape, F32) for shap...]
where the time goes in v2:
time: 53.5 us; the launch traced here: 53.4 us
  Pallas kernels  52.7 us (99%)
  between operations  0.64 us (1%)
    pallas_call x1, Pallas kernels, per_device(): pl.pallas_call(kernel, out_shape=(pltpu.VMEM((ROWS, NDEV), F32), pltpu.VM...  51.2 us
    pallas_call x1, Pallas kernels, per_device(): pl.pallas_call(write_out, out_shape=tuple((pltpu.HBM(shape, F32) for shap...  1.48 us

profile of v2, /device:TPU:1, one launch (start us, length us, event | category | flops | bytes accessed | tf_op | source)
XLA Modules:
  0.0 53.4 jit_solution(7477593776342323349)
XLA Ops:
  0.6 51.2 %shard_map.120 = (f32[4536,128]{1,0:T(8,128)S(1)}, f32[3,1,2,8]{3,2,1,0:T(2,128)S(1)}, f32[3,1,2,8]{3,2,1,0:T(2,128)S(1)}, f32[8,128]{1,0:T(8,128)S(1)}) custom-call(f32[3,1,2,8]{3,2,1,0:T(2,128)} %disp_hbm.1, f32[3,1,2,8]{3,2,1,0:T(2,128)} %load_hbm.1, s32[1,128]{1,0:T(1,128)} %bitcast.7, s32[1,128]{1,0:T(1,128)} %bitcast.8, f32[2,3]{1,0:T(2,128)} %moduli_hbm.1, ...), custom_call_target="tpu_custom_call" | custom-call | tf_op jit(solution)/shard_map/pallas_call | solution.py:623
  51.9 1.5 %shard_map.121 = (f32[4536,128]{1,0:T(8,128)}, f32[3,1,2,8]{3,2,1,0:T(2,128)}, f32[3,1,2,8]{3,2,1,0:T(2,128)}, f32[1,128]{1,0:T(1,128)}) custom-call(f32[4536,128]{1,0:T(8,128)S(1)} %get-tuple-element.12.new_vmem, f32[3,1,2,8]{3,2,1,0:T(2,128)S(1)} %get-tuple-element.13.displaced_vmem, f32[3,1,2,8]{3,2,1,0:T(2,128)S(1)} %get-tuple-element.14.residual_vmem, ...), custom_call_target="tpu_custom_call" | custom-call | tf_op jit(solution)/shard_map/pallas_call | solution.py:677

commit v3 on v2

--- a/solution.py
+++ b/solution.py
@@ -1,4 +1,4 @@
-import functools
+import itertools
 import math
 
 import jax
@@ -26,11 +26,13 @@
 MACRO = 2
 STRAIN_ROW = 3 * CASE_ROWS
 STRESS_ROW = 7 * CASE_ROWS + 8
-RETURN, NORM = LAST + 1, LAST + 2
+RESULT = LAST + 1
 CELLS = 36
 LOGICAL = pl.DeviceIdType.LOGICAL
 F32 = jnp.float32
 TERMS = (((0, 0), (2, 4), (1, 5)), ((1, 1), (2, 3), (0, 5)), ((2, 2), (1, 3), (0, 4)))
+ENTRIES = [(m, m) for m in range(6)]
+ENTRIES += [(min(t[0][1], t[1][1]), max(t[0][1], t[1][1])) for i in range(3) for t in itertools.combinations(TERMS[i], 2)]
 
 
 def tables():
@@ -63,8 +65,14 @@
         for a in range(8):
             ax, ay, az = a % 2, a // 2 % 2, a // 4
             corner[a, g] = az * 24 + (ly + ay) * 8 + (ex + ax) % 8
+    own = np.zeros((8, NDEV), np.int32)
+    for n in range(16):
+        ny, nx = n // 8, n % 8
+        for a in range(8):
+            ax, ay = a % 2, a // 2 % 2
+            own[a, n] = ((1 - ny if ay else ny) * 8 + (nx - ax) % 8) * 8
     floats = np.concatenate([slopes.reshape(24, NDEV), mask], axis=0)
-    ints = np.concatenate([pick, corner], axis=0)
+    ints = np.concatenate([pick, corner, own], axis=0)
     return floats, ints
 
 
@@ -103,7 +111,7 @@
     disp_hbm, load_hbm, home_hbm, state_hbm, moduli_hbm, float_hbm, int_hbm, micro_ref, phase_ref,
     new_ref, displaced_ref, residual_ref, norm_ref,
     disp_ref, load_ref, home_ref, state_slot_ref, moduli_ref, float_ref, int_ref, xin, ph, send0, send1, send2, send3, send4, send5, send6, recv0, recv1, recv2, recv3, recv4, recv5, recv6,
-    nat, lam, mu, w, p0, p1, ap, sig, keep, av, ret_out, ret_in, dtile, dhalo, ntile, nhalo, nrow, nall, whole_residual,
+    nat, lam, mu, w, p0, p1, ap, sig, keep, av, rows_out, rows_in, dtile, dhalo, home_near, spare, whole_residual,
     small_sem, in_sem, ph_sem, local_sem, send_sem, recv_sem, near_send, near_recv,
 ):
     sub, rve = lax.axis_index("sub"), lax.axis_index("rve")
@@ -218,6 +226,7 @@
 
     steps = ((0, 1), (1, 0), (1, 1))
     halo_in = [near(i, dtile, dhalo.at[i], -s, -r) for i, (s, r) in enumerate(steps)]
+    halo_in += [near(3 + i, home_ref, home_near.at[i], s, r) for i, (s, r) in enumerate(steps)]
     for copy in halo_in:
         copy.start()
     send_chunk(0)
@@ -369,7 +378,7 @@
             tile = jnp.where(row8 == r, spread(value), tile)
         return tile
 
-    def assemble_force():
+    def residual_part():
         stress = lanes(nat[pl.ds(STRESS_ROW, 8), :], home_rows)
         rows = []
         for i in range(3):
@@ -381,10 +390,8 @@
         load_square = jnp.sum(load_rows * load_rows, keepdims=True)
         part = load_rows - tiled(rows)
         first_row = part[0:1] + pltpu.roll(part[1:2], 64, axis=1)
-        second_row = jnp.where(lane[0:1] == NDEV - 1, jnp.broadcast_to(load_square, (1, NDEV)), part[2:3])
-        both = jnp.concatenate([first_row, second_row], axis=0)
-        nrow[...] = both
-        nall[pl.ds(me * 2, 2), :] = both
+        second_row = jnp.where(lane[0:1] == 63, jnp.broadcast_to(load_square, (1, NDEV)), part[2:3])
+        return spread(first_row), spread(second_row)
 
     def case_body(position, carry):
         for chunk in range(CASES):
@@ -487,58 +494,64 @@
 
     lax.fori_loop(0, CASES, case_body, 0)
 
-    def send_rows(src, dst, rows, index):
-        own = pl.ds(me * rows, rows)
-        for d in others(FARTHEST):
-            pltpu.make_async_remote_copy(
-                src_ref=src.at[pl.ds(d, 1)] if index == RETURN else src,
-                dst_ref=dst.at[own],
-                send_sem=send_sem.at[index],
-                recv_sem=recv_sem.at[index],
-                device_id=d,
-                device_id_type=LOGICAL,
-            ).start()
-
-    ret_out[...] = av[...].T
-    send_rows(ret_out, ret_in, 1, RETURN)
-    own_row = pl.ds(me, 1)
-    own_copy = pltpu.make_async_copy(ret_out.at[own_row], ret_in.at[own_row], local_sem.at[RETURN])
+    for r, (m, j) in enumerate(ENTRIES):
+        entry = av[(1 + j) * 6 + m : (1 + j) * 6 + m + 1, :]
+        if m != j:
+            entry = entry + av[(1 + m) * 6 + j : (1 + m) * 6 + j + 1, :]
+        spare[r : r + 1, :] = entry
+    spare[15:16, :] = jnp.zeros((1, NDEV), F32)
+    step_back = lax.rem(lane + 3, 4) - lax.rem(lane, 4) + lane
+    here = [spare[0:8, :], spare[8:16, :]]
+    beside = [lanes(x, step_back) for x in here]
+    under = [pltpu.roll(x, NRVE, axis=1) for x in here + beside]
+    back_rows = jnp.concatenate([zero] * 8 + here + beside + under, axis=0).T
+    first_row, second_row = residual_part()
+    for block in range(16):
+        rows_out[pl.ds(block * 16, 8, stride=2), :] = first_row
+        rows_out[pl.ds(block * 16 + 1, 8, stride=2), :] = back_rows[8 * block : 8 * block + 8, :] + second_row
+    own = pl.ds(me * 2, 2)
+    for d in others(FARTHEST):
+        pltpu.make_async_remote_copy(
+            src_ref=rows_out.at[pl.ds(d * 2, 2)],
+            dst_ref=rows_in.at[own],
+            send_sem=send_sem.at[RESULT],
+            recv_sem=recv_sem.at[RESULT],
+            device_id=d,
+            device_id_type=LOGICAL,
+        ).start()
+    own_copy = pltpu.make_async_copy(rows_out.at[own], rows_in.at[own], local_sem.at[RESULT])
     own_copy.start()
-    assemble_force()
-    send_rows(nrow, nall, 2, NORM)
     finish(ORDER[LAST])
-    whole(ret_out, ret_in, 1, RETURN).wait_recv()
+    whole(rows_out, rows_in, 2, RESULT).wait_recv()
     own_copy.wait()
-    back = ret_in[...].T
-    at_home = [lanes(back[8 * i : 8 * i + 8, :], home_rows) for i in range(6)]
-
-    def tangent(m, j):
-        row = (1 + j) * 6 + m
-        return at_home[row // 8][row % 8 : row % 8 + 1, :]
-
+    back = rows_in[pl.ds(1, NDEV, stride=2), :].T
+    above = jnp.where(sub > 0, 1.0, 0.0).astype(F32)
+    targets = [home_rows] + [spread(lax.shift_right_logical(home_near[b], 7)) for b in range(3)]
+    product = {(k, l): grad[k] * grad[l] for k in range(3) for l in range(k, 3)}
+    parts = []
+    for b in range(4):
+        found = [lanes(back[64 + 16 * b + 8 * h : 64 + 16 * b + 8 * h + 8, :], targets[b]) for h in range(2)]
+        values = []
+        for i in range(3):
+            value = zero
+            for (k, m), (l, j) in itertools.combinations_with_replacement(TERMS[i], 2):
+                r = ENTRIES.index((min(m, j), max(m, j)))
+                value = value + product[min(k, l), max(k, l)] * spread(found[r // 8][r % 8 : r % 8 + 1, :])
+            values.append(value)
+        parts.append(values)
+    lower = row8 < 4
+    crossing = (lax.rem(row8, 4) >= 2) & (lane >= 64)
     diagonal = []
     for i in range(3):
-        value = zero
-        for k, m in TERMS[i]:
-            inner = zero
-            for l, j in TERMS[i]:
-                inner = inner + grad[l] * tangent(m, j)
-            value = value + grad[k] * inner
-        diagonal.append(to_nodes(value))
-    tile = tiled(diagonal)
-    ntile[...] = tile
-    halo_out = [near(3 + i, ntile, nhalo.at[i], s, r) for i, (s, r) in enumerate(steps)]
-    for copy in halo_out:
-        copy.start()
-
-    pltpu.make_async_remote_copy(
-        src_ref=nall.at[pl.ds(0, 2 * NDEV - 2)],
-        dst_ref=nall.at[pl.ds(0, 2 * NDEV - 2)],
-        send_sem=send_sem.at[NORM],
-        recv_sem=recv_sem.at[NORM],
-        device_id=other,
-        device_id_type=LOGICAL,
-    ).wait_recv()
+        inner = jnp.where(lower, parts[0][i], parts[2][i] * above)
+        outer = jnp.where(lower, parts[1][i], parts[3][i] * above)
+        value = jnp.where(crossing, outer, inner)
+        for step in (1, 2, 4):
+            value = value + pltpu.roll(value, NDEV - step, axis=1)
+        value = lanes(value, int_ref[16:24, :]) * 0.125
+        diagonal.append(jnp.sum(value, axis=0, keepdims=True))
+    node = tiled(diagonal)
+
     turn = jnp.where(lax.rem(row8, 4) == 0, row8 + 3, row8 - 1)
     square = zero
     load_sum = zero
@@ -546,12 +559,12 @@
     for half in range(2):
         before_z = zero
         for block in range(16):
-            value = nall[pl.ds(block * 16 + half, 8, stride=2), :]
+            value = rows_in[pl.ds(block * 16 + half, 8, stride=2), :]
             if half == 1:
-                load_sum = load_sum + jnp.where(lane == NDEV - 1, value, 0.0)
-                value = jnp.where(lane < 64, value, 0.0)
-            other = pltpu.roll(sublanes(value, turn), NDEV - 16, axis=1)
-            value = value + jnp.where((low < 8) | ((low >= 24) & (low < 32)), other, 0.0)
+                load_sum = load_sum + jnp.where(lane == 63, value, 0.0)
+                value = jnp.where(lane < 48, value, 0.0)
+            before = pltpu.roll(sublanes(value, turn), NDEV - 16, axis=1)
+            value = value + jnp.where((low < 8) | ((low >= 24) & (low < 32)), before, 0.0)
             plane = pltpu.roll(value, NDEV - 24, axis=1)
             shifted = jnp.where(row8 < 4, pltpu.roll(before_z, 4, axis=0), pltpu.roll(plane, 4, axis=0))
             before_z = plane
@@ -561,13 +574,6 @@
     ratio = jnp.sqrt(jnp.sum(square, keepdims=True) / jnp.sum(load_sum, keepdims=True))
     norm_ref[...] = jnp.broadcast_to(ratio, (8, NDEV))
 
-    for copy in halo_out:
-        copy.wait()
-    above = jnp.where(sub > 0, 1.0, 0.0).astype(F32)
-    node = jnp.where(lane < 16, tile, 0.0)
-    node = node + jnp.where(lane < 8, pltpu.roll(nhalo[0], NDEV - 16, axis=1), 0.0)
-    node = node + jnp.where(lane < 16, pltpu.roll(nhalo[1], NDEV - 24, axis=1) * above, 0.0)
-    node = node + jnp.where(lane < 8, pltpu.roll(nhalo[2], NDEV - 40, axis=1) * above, 0.0)
     pair = whole_residual[0, pl.ds(me, 1), :]
     residual = jnp.concatenate([pair, pltpu.roll(pair, 64, axis=1), whole_residual[1, pl.ds(me, 1), :]], axis=0)
     moved = dtile[0:3, :] + residual / jnp.maximum(node[0:3], FLOOR)
@@ -578,15 +584,7 @@
 
     for chunk in range(CASES):
         whole(sends[chunk], recvs[chunk], CHUNKS[chunk], chunk).wait_send()
-    whole(ret_out, ret_in, 1, RETURN).wait_send()
-    pltpu.make_async_remote_copy(
-        src_ref=nall.at[pl.ds(0, 2 * NDEV - 2)],
-        dst_ref=nall.at[pl.ds(0, 2 * NDEV - 2)],
-        send_sem=send_sem.at[NORM],
-        recv_sem=recv_sem.at[NORM],
-        device_id=other,
-        device_id_type=LOGICAL,
-    ).wait_send()
+    whole(rows_out, rows_in, 2, RESULT).wait_send()
 
 
 def write_out(new_vmem, displaced_vmem, residual_vmem, norm_vmem, new_ref, displaced_ref, residual_ref, norm_ref, sem):
@@ -652,21 +650,19 @@
             pltpu.VMEM((6 * CELLS, 8, NDEV), F32),
             pltpu.VMEM((2, 8, NDEV), F32),
             pltpu.VMEM((NDEV, NDEV), F32),
-            pltpu.VMEM((NDEV, NDEV), F32),
-            pltpu.VMEM((NDEV, NDEV), F32),
+            pltpu.VMEM((2 * NDEV, NDEV), F32),
+            pltpu.VMEM((2 * NDEV, NDEV), F32),
             pltpu.VMEM((8, NDEV), F32),
             pltpu.VMEM((4, 8, NDEV), F32),
-            pltpu.VMEM((8, NDEV), F32),
-            pltpu.VMEM((3, 8, NDEV), F32),
-            pltpu.VMEM((2, NDEV), F32),
-            pltpu.VMEM((2 * NDEV, NDEV), F32),
+            pltpu.VMEM((3, 1, NDEV), jnp.int32),
+            pltpu.VMEM((16, NDEV), F32),
             pltpu.VMEM((2, NDEV, NDEV), F32),
             dma((7,)),
             dma((CASES,)),
             dma,
             dma((CASES + 1,)),
-            dma((CASES + 2,)),
-            dma((CASES + 2,)),
+            dma((CASES + 1,)),
+            dma((CASES + 1,)),
             dma((6,)),
             dma((6,)),
         ],

time: 53.5 us -> 51.3 us (0.959)
  Pallas kernels: 52.7 us -> 50.5 us
    pallas_call x1, Pallas kernels: 51.2 us -> 49 us  [per_device(): pl.pallas_call(kernel, out_shape=(pltpu.VMEM((ROWS, NDEV), F32), pltpu.VM...]
where the time goes in v3:
time: 51.3 us; the launch traced here: 51.1 us
  Pallas kernels  50.5 us (98%)
  between operations  0.64 us (1%)
    pallas_call x1, Pallas kernels, per_device(): pl.pallas_call(kernel, out_shape=(pltpu.VMEM((ROWS, NDEV), F32), pltpu.VM...  49 us
    pallas_call x1, Pallas kernels, per_device(): pl.pallas_call(write_out, out_shape=tuple((pltpu.HBM(shape, F32) for shap...  1.48 us

profile of v3, /device:TPU:1, one launch (start us, length us, event | category | flops | bytes accessed | tf_op | source)
XLA Modules:
  0.0 51.1 jit_solution(2202569761618946923)
XLA Ops:
  0.6 49.0 %shard_map.120 = (f32[4536,128]{1,0:T(8,128)S(1)}, f32[3,1,2,8]{3,2,1,0:T(2,128)S(1)}, f32[3,1,2,8]{3,2,1,0:T(2,128)S(1)}, f32[8,128]{1,0:T(8,128)S(1)}) custom-call(f32[3,1,2,8]{3,2,1,0:T(2,128)} %disp_hbm.1, f32[3,1,2,8]{3,2,1,0:T(2,128)} %load_hbm.1, s32[1,128]{1,0:T(1,128)} %bitcast.7, s32[1,128]{1,0:T(1,128)} %bitcast.8, f32[2,3]{1,0:T(2,128)} %moduli_hbm.1, ...), custom_call_target="tpu_custom_call" | custom-call | tf_op jit(solution)/shard_map/pallas_call | solution.py:621
  49.7 1.5 %shard_map.121 = (f32[4536,128]{1,0:T(8,128)}, f32[3,1,2,8]{3,2,1,0:T(2,128)}, f32[3,1,2,8]{3,2,1,0:T(2,128)}, f32[1,128]{1,0:T(1,128)}) custom-call(f32[4536,128]{1,0:T(8,128)S(1)} %get-tuple-element.12.new_vmem, f32[3,1,2,8]{3,2,1,0:T(2,128)S(1)} %get-tuple-element.13.displaced_vmem, f32[3,1,2,8]{3,2,1,0:T(2,128)S(1)} %get-tuple-element.14.residual_vmem, ...), custom_call_target="tpu_custom_call" | custom-call | tf_op jit(solution)/shard_map/pallas_call | solution.py:673

commit v4 on v3

--- a/solution.py
+++ b/solution.py
@@ -185,7 +185,7 @@
     def send_chunk(chunk):
         rows = CHUNKS[chunk]
         own = pl.ds(me * rows, rows)
-        for d in others(SPREAD):
+        for d in others(FARTHEST if chunk == LAST else SPREAD):
             pltpu.make_async_remote_copy(
                 src_ref=sends[chunk].at[pl.ds(d * rows, rows)],
                 dst_ref=recvs[chunk].at[own],
@@ -297,7 +297,7 @@
     zero = jnp.zeros((8, NDEV), F32)
 
     def stress_at(src, a, b, applied):
-        following = lax.rem(a + 1, R)
+        following = (a + 1) % R
         g = []
         for i in range(3):
             here = src[i * CELLS + a * R + b]
@@ -328,12 +328,12 @@
                     total[m] = total[m] + stress[m]
             return tuple(total)
 
-        return lax.fori_loop(0, R, body, (zero,) * 6)
+        return sweep(body, (zero,) * 6)
 
     voigt = ((0, 5, 4), (5, 1, 3), (4, 3, 2))
 
     def force_at(src, a, b):
-        before = lax.rem(a + R - 1, R)
+        before = (a + R - 1) % R
         cell = a * R + b
         here = [sig[m * CELLS + cell] for m in range(6)]
         out = []
@@ -344,6 +344,11 @@
             total = total + (sublanes(last, down) - last)
             out.append(total + STAB * src[i * CELLS + cell])
         return out
+
+    def sweep(body, carry):
+        for a in range(R):
+            carry = body(a, carry)
+        return carry
 
     def across(x):
         return spread(jnp.sum(x, axis=0, keepdims=True))
@@ -408,12 +413,10 @@
             unit = jnp.where(case == m + 1, 1.0, 0.0).astype(F32)
             applied.append(jnp.where(position == MACRO, spread(macro[m : m + 1, :]), unit))
 
-        @pl.loop(0, R)
-        def _(a):
+        start = base_of(position)
+        for cell in range(CELLS):
             for i in range(3):
-                at = base_of(position) + i * VOX + a * (R * R)
-                for b in range(R):
-                    w[i * CELLS + a * R + b] = jnp.where(inside, nat[pl.ds(at + b * R, 8), :], 0.0)
+                w[i * CELLS + cell] = jnp.where(inside, nat[pl.ds(start + i * VOX + cell * R, 8), :], 0.0)
 
         total0 = stresses(w, applied)
 
@@ -427,7 +430,7 @@
                 rr = rr + (force[0] + (force[1] + force[2]))
             return rr
 
-        rr = across(lax.fori_loop(0, R, first, zero))
+        rr = across(sweep(first, zero))
         total1 = stresses(p0, None)
 
         def second(a, curve):
@@ -439,7 +442,7 @@
                 curve = curve + (force[0] + (force[1] + force[2]))
             return curve
 
-        alpha0 = rr / across(lax.fori_loop(0, R, second, zero))
+        alpha0 = rr / across(sweep(second, zero))
 
         def reduce(a, total):
             total = list(total)
@@ -450,15 +453,12 @@
                 total[j % 6] = total[j % 6] + value * value
             return tuple(total)
 
-        parts = lax.fori_loop(0, R, reduce, (zero,) * 6)
+        parts = sweep(reduce, (zero,) * 6)
         rn = across(((parts[0] + parts[1]) + (parts[2] + parts[3])) + (parts[4] + parts[5]))
         beta = rn / rr
 
-        @pl.loop(0, R)
-        def _(a):
-            for j in range(3 * R):
-                at = a * (3 * R) + j
-                p1[at] = p1[at] + beta * p0[at]
+        for at in range(3 * CELLS):
+            p1[at] = p1[at] + beta * p0[at]
 
         def third(a, carried):
             curve, total = carried[0], list(carried[1:])
@@ -472,7 +472,7 @@
                 curve = curve + (((work[0] + work[1]) + (work[2] + work[3])) + ((work[4] + work[5]) + kept))
             return (curve, *total)
 
-        found = lax.fori_loop(0, R, third, (zero,) * 7)
+        found = sweep(third, (zero,) * 7)
         alpha1 = rn / across(found[0])
         for m in range(6):
             mean = jnp.sum(total0[m] + alpha0 * total1[m] + alpha1 * found[1 + m], axis=0, keepdims=True)

time: 51.3 us -> 50.3 us (0.981)
  Pallas kernels: 50.5 us -> 49.5 us
    pallas_call x1, Pallas kernels: 49 us -> 48 us  [per_device(): pl.pallas_call(kernel, out_shape=(pltpu.VMEM((ROWS, NDEV), F32), pltpu.VM...]
where the time goes in v4:
time: 50.3 us; the launch traced here: 50.2 us
  Pallas kernels  49.5 us (98%)
  between operations  0.64 us (1%)
    pallas_call x1, Pallas kernels, per_device(): pl.pallas_call(kernel, out_shape=(pltpu.VMEM((ROWS, NDEV), F32), pltpu.VM...  48 us
    pallas_call x1, Pallas kernels, per_device(): pl.pallas_call(write_out, out_shape=tuple((pltpu.HBM(shape, F32) for shap...  1.48 us

profile of v4, /device:TPU:1, one launch (start us, length us, event | category | flops | bytes accessed | tf_op | source)
XLA Modules:
  0.0 50.2 jit_solution(16970911409917123018)
XLA Ops:
  0.6 48.0 %shard_map.120 = (f32[4536,128]{1,0:T(8,128)S(1)}, f32[3,1,2,8]{3,2,1,0:T(2,128)S(1)}, f32[3,1,2,8]{3,2,1,0:T(2,128)S(1)}, f32[8,128]{1,0:T(8,128)S(1)}) custom-call(f32[3,1,2,8]{3,2,1,0:T(2,128)} %disp_hbm.1, f32[3,1,2,8]{3,2,1,0:T(2,128)} %load_hbm.1, s32[1,128]{1,0:T(1,128)} %bitcast.7, s32[1,128]{1,0:T(1,128)} %bitcast.8, f32[2,3]{1,0:T(2,128)} %moduli_hbm.1, ...), custom_call_target="tpu_custom_call" | custom-call | tf_op jit(solution)/shard_map/pallas_call | solution.py:621
  48.7 1.5 %shard_map.121 = (f32[4536,128]{1,0:T(8,128)}, f32[3,1,2,8]{3,2,1,0:T(2,128)}, f32[3,1,2,8]{3,2,1,0:T(2,128)}, f32[1,128]{1,0:T(1,128)}) custom-call(f32[4536,128]{1,0:T(8,128)S(1)} %get-tuple-element.12.new_vmem, f32[3,1,2,8]{3,2,1,0:T(2,128)S(1)} %get-tuple-element.13.displaced_vmem, f32[3,1,2,8]{3,2,1,0:T(2,128)S(1)} %get-tuple-element.14.residual_vmem, ...), custom_call_target="tpu_custom_call" | custom-call | tf_op jit(solution)/shard_map/pallas_call | solution.py:673

commit v5 on v4

--- a/solution.py
+++ b/solution.py
@@ -418,6 +418,7 @@
             for i in range(3):
                 w[i * CELLS + cell] = jnp.where(inside, nat[pl.ds(start + i * VOX + cell * R, 8), :], 0.0)
 
+        keep[2], keep[3] = residual_part()
         total0 = stresses(w, applied)
 
         def first(a, rr):
@@ -505,7 +506,7 @@
     beside = [lanes(x, step_back) for x in here]
     under = [pltpu.roll(x, NRVE, axis=1) for x in here + beside]
     back_rows = jnp.concatenate([zero] * 8 + here + beside + under, axis=0).T
-    first_row, second_row = residual_part()
+    first_row, second_row = keep[2], keep[3]
     for block in range(16):
         rows_out[pl.ds(block * 16, 8, stride=2), :] = first_row
         rows_out[pl.ds(block * 16 + 1, 8, stride=2), :] = back_rows[8 * block : 8 * block + 8, :] + second_row
@@ -546,10 +547,10 @@
         inner = jnp.where(lower, parts[0][i], parts[2][i] * above)
         outer = jnp.where(lower, parts[1][i], parts[3][i] * above)
         value = jnp.where(crossing, outer, inner)
-        for step in (1, 2, 4):
-            value = value + pltpu.roll(value, NDEV - step, axis=1)
-        value = lanes(value, int_ref[16:24, :]) * 0.125
-        diagonal.append(jnp.sum(value, axis=0, keepdims=True))
+        points = [lanes(value, int_ref[16:24, :] + q) for q in range(8)]
+        while len(points) > 1:
+            points = [x + y for x, y in zip(points[::2], points[1::2])]
+        diagonal.append(jnp.sum(points[0] * 0.125, axis=0, keepdims=True))
     node = tiled(diagonal)
 
     turn = jnp.where(lax.rem(row8, 4) == 0, row8 + 3, row8 - 1)
@@ -648,7 +649,7 @@
             cells,
             cells,
             pltpu.VMEM((6 * CELLS, 8, NDEV), F32),
-            pltpu.VMEM((2, 8, NDEV), F32),
+            pltpu.VMEM((4, 8, NDEV), F32),
             pltpu.VMEM((NDEV, NDEV), F32),
             pltpu.VMEM((2 * NDEV, NDEV), F32),
             pltpu.VMEM((2 * NDEV, NDEV), F32),

time: 50.3 us -> 50 us (level)
  no operation moved by 1% of the time
where the time goes in v5:
time: 50 us; the launch traced here: 49.9 us
  Pallas kernels  49.2 us (98%)
  between operations  0.64 us (1%)
    pallas_call x1, Pallas kernels, per_device(): pl.pallas_call(kernel, out_shape=(pltpu.VMEM((ROWS, NDEV), F32), pltpu.VM...  47.8 us
    pallas_call x1, Pallas kernels, per_device(): pl.pallas_call(write_out, out_shape=tuple((pltpu.HBM(shape, F32) for shap...  1.48 us

profile of v5, /device:TPU:1, one launch (start us, length us, event | category | flops | bytes accessed | tf_op | source)
XLA Modules:
  0.0 49.9 jit_solution(13629077013263500534)
XLA Ops:
  0.6 47.8 %shard_map.120 = (f32[4536,128]{1,0:T(8,128)S(1)}, f32[3,1,2,8]{3,2,1,0:T(2,128)S(1)}, f32[3,1,2,8]{3,2,1,0:T(2,128)S(1)}, f32[8,128]{1,0:T(8,128)S(1)}) custom-call(f32[3,1,2,8]{3,2,1,0:T(2,128)} %disp_hbm.1, f32[3,1,2,8]{3,2,1,0:T(2,128)} %load_hbm.1, s32[1,128]{1,0:T(1,128)} %bitcast.7, s32[1,128]{1,0:T(1,128)} %bitcast.8, f32[2,3]{1,0:T(2,128)} %moduli_hbm.1, ...), custom_call_target="tpu_custom_call" | custom-call | tf_op jit(solution)/shard_map/pallas_call | solution.py:622
  48.4 1.5 %shard_map.121 = (f32[4536,128]{1,0:T(8,128)}, f32[3,1,2,8]{3,2,1,0:T(2,128)}, f32[3,1,2,8]{3,2,1,0:T(2,128)}, f32[1,128]{1,0:T(1,128)}) custom-call(f32[4536,128]{1,0:T(8,128)S(1)} %get-tuple-element.12.new_vmem, f32[3,1,2,8]{3,2,1,0:T(2,128)S(1)} %get-tuple-element.13.displaced_vmem, f32[3,1,2,8]{3,2,1,0:T(2,128)S(1)} %get-tuple-element.14.residual_vmem, ...), custom_call_target="tpu_custom_call" | custom-call | tf_op jit(solution)/shard_map/pallas_call | solution.py:674
